TPU v7x, 8 devices: a whole 2x2x1 slice. The times are simulated.
8 devices in a mesh: dp: 2 (over z, y), stage: 4 (over x, core).
Axes of the slice: x: 2, y: 2, z: 1, core: 2. Of those that a mesh axis runs over, the one named last changes fastest.
Arguments:
- token_ids: int32 [32, 512], P('dp'), parts along dimension 0
- label_ids: int32 [32, 512], P('dp'), parts along dimension 0
- embedding: bfloat16 [50304, 768], P('stage')
- w_in: bfloat16 [4, 768, 3072], P('stage')
- w_out: bfloat16 [4, 3072, 768], P('stage')
Outputs:
- output 1: float32 [2], P('dp'), parts along dimension 0
- output 2: float32 [8, 768, 3072], P(('dp', 'stage')), parts along dimension 0
- output 3: float32 [8, 3072, 768], P(('dp', 'stage')), parts along dimension 0
- output 4: float32 [100608, 768], P(('dp', 'stage')), parts along dimension 0
There are 2 independent parts. A program takes and returns all parts, laid end to end along the dimension named above; an argument that names none is the same for every part.
All inputs are finite; a program needn't handle non-finite values.
Results may differ from a plain program's by a relative error of at most 0.00981087.
Values are sent between devices in bfloat16 or wider.
A program may use at most 1 GiB of HBM per device.

v0:
```python
import jax
import jax.numpy as jnp
from jax import lax
from jax.sharding import PartitionSpec as P

NORM_EPS = 1e-6


def norm_f32(act_rows):
    acts_f = act_rows.astype(jnp.float32)
    return acts_f * lax.rsqrt(jnp.mean(acts_f * acts_f, axis=-1, keepdims=True) + NORM_EPS)


def layer_forward(act_rows, w_first, w_second):
    pre_act = jnp.dot(act_rows, w_first, preferred_element_type=jnp.float32)
    hidden = jax.nn.gelu(pre_act).astype(jnp.bfloat16)
    out_f = act_rows.astype(jnp.float32) + jnp.dot(hidden, w_second, preferred_element_type=jnp.float32)
    return out_f.astype(jnp.bfloat16)


def layer_backward(act_rows, grad_out, w_first, w_second):
    pre_act = jnp.dot(act_rows, w_first, preferred_element_type=jnp.float32)
    hidden_f, gelu_pull = jax.vjp(jax.nn.gelu, pre_act)
    hidden = hidden_f.astype(jnp.bfloat16)
    grad_second = jnp.einsum("tf,td->fd", hidden, grad_out, preferred_element_type=jnp.float32)
    grad_hidden = jnp.einsum("td,fd->tf", grad_out, w_second, preferred_element_type=jnp.float32)
    grad_pre = gelu_pull(grad_hidden)[0].astype(jnp.bfloat16)
    grad_first = jnp.einsum("td,tf->df", act_rows, grad_pre, preferred_element_type=jnp.float32)
    grad_in = (grad_out.astype(jnp.float32) + jnp.einsum("tf,df->td", grad_pre, w_first, preferred_element_type=jnp.float32)).astype(jnp.bfloat16)
    return grad_in, grad_first, grad_second


def take_slot(store_arr, mb_slot):
    return lax.dynamic_index_in_dim(store_arr, mb_slot, 0, keepdims=False)


def put_slot(store_arr, new_value, mb_slot, active):
    old_value = lax.dynamic_index_in_dim(store_arr, mb_slot, 0, keepdims=False)
    return lax.dynamic_update_index_in_dim(store_arr, jnp.where(active, new_value, old_value), mb_slot, 0)


def solution(mesh):
    n_stage = mesh.shape["stage"]
    fwd_pairs = [(src_idx, src_idx + 1) for src_idx in range(n_stage - 1)]
    bwd_pairs = [(src_idx + 1, src_idx) for src_idx in range(n_stage - 1)]

    def stage_body(token_ids, label_ids, emb_rows, w_in, w_out):
        stage_idx = lax.axis_index("stage")
        is_first = stage_idx == 0
        is_last = stage_idx == n_stage - 1
        micro_count, micro_tokens = token_ids.shape
        slice_rows, model_dim = emb_rows.shape
        logit_scale = model_dim ** -0.5
        w_first = w_in[0]
        w_second = w_out[0]
        n_ticks = micro_count + n_stage - 1
        row_start = stage_idx * slice_rows
        local_tok = token_ids - row_start
        tok_here = (local_tok >= 0) & (local_tok < slice_rows)
        looked_up = jnp.take(emb_rows, jnp.clip(local_tok, 0, slice_rows - 1), axis=0)
        embedded = lax.psum(jnp.where(tok_here[..., None], looked_up, 0), "stage")
        act_zeros = jnp.zeros((micro_tokens, model_dim), jnp.bfloat16)
        store_zeros = jnp.zeros((micro_count, micro_tokens, model_dim), jnp.bfloat16)

        def fwd_tick(tick_idx, loop_carry):
            incoming, saved_in, last_out = loop_carry
            micro_idx = tick_idx - stage_idx
            active = (micro_idx >= 0) & (micro_idx < micro_count)
            mb_slot = jnp.clip(micro_idx, 0, micro_count - 1)
            act_in = jnp.where(is_first, take_slot(embedded, mb_slot), incoming)
            act_out = lax.cond(active, lambda act_val: layer_forward(act_val, w_first, w_second), lambda act_val: act_val, act_in)
            saved_in = put_slot(saved_in, act_in, mb_slot, active)
            last_out = put_slot(last_out, act_out, mb_slot, active)
            return lax.ppermute(act_out, "stage", fwd_pairs), saved_in, last_out

        _, saved_in, last_out = lax.fori_loop(0, n_ticks, fwd_tick, (act_zeros, store_zeros, store_zeros))

        normed_f, norm_pull = jax.vjp(norm_f32, last_out)
        normed = lax.psum(jnp.where(is_last, normed_f.astype(jnp.bfloat16), 0), "stage")
        local_lab = label_ids - row_start
        vocab_iota = jnp.arange(slice_rows, dtype=jnp.int32)

        def head_step(loop_carry, inputs):
            grad_rows, loss_sum = loop_carry
            normed_mb, lab_mb = inputs
            logits = jnp.einsum("td,vd->tv", normed_mb, emb_rows, preferred_element_type=jnp.float32) * logit_scale
            row_max = lax.pmax(jnp.max(logits, axis=1), "stage")
            exp_logits = jnp.exp(logits - row_max[:, None])
            is_label = lab_mb[:, None] == vocab_iota[None, :]
            row_stats = lax.psum(jnp.stack([jnp.sum(exp_logits, axis=1), jnp.sum(jnp.where(is_label, logits, 0.0), axis=1)]), "stage")
            loss_sum = loss_sum + jnp.sum(jnp.log(row_stats[0]) + row_max - row_stats[1])
            grad_logits = ((exp_logits / row_stats[0][:, None] - is_label.astype(jnp.float32)) * logit_scale).astype(jnp.bfloat16)
            grad_n = lax.psum(jnp.einsum("tv,vd->td", grad_logits, emb_rows, preferred_element_type=jnp.float32), "stage")
            grad_rows = grad_rows + jnp.einsum("tv,td->vd", grad_logits, normed_mb, preferred_element_type=jnp.float32)
            return (grad_rows, loss_sum), grad_n

        head_init = (jnp.zeros((slice_rows, model_dim), jnp.float32), jnp.zeros((), jnp.float32))
        (grad_head, loss_sum), grad_norm = lax.scan(head_step, head_init, (normed, local_lab))
        grad_last = norm_pull(grad_norm)[0]

        def run_layer(operands):
            act_rows, grad_val, acc_a, acc_b = operands
            grad_in, grad_a, grad_b = layer_backward(act_rows, grad_val, w_first, w_second)
            return grad_in, acc_a + grad_a, acc_b + grad_b

        def skip_layer(operands):
            return operands[1], operands[2], operands[3]

        def bwd_tick(tick_idx, loop_carry):
            incoming, acc_first, acc_second, grad_embedded = loop_carry
            micro_idx = tick_idx - (n_stage - 1 - stage_idx)
            active = (micro_idx >= 0) & (micro_idx < micro_count)
            mb_slot = jnp.clip(micro_idx, 0, micro_count - 1)
            grad_out = jnp.where(is_last, take_slot(grad_last, mb_slot), incoming)
            grad_in, acc_first, acc_second = lax.cond(active, run_layer, skip_layer, (take_slot(saved_in, mb_slot), grad_out, acc_first, acc_second))
            grad_embedded = put_slot(grad_embedded, grad_in, mb_slot, active)
            return lax.ppermute(grad_in, "stage", bwd_pairs), acc_first, acc_second, grad_embedded

        bwd_init = (act_zeros, jnp.zeros(w_first.shape, jnp.float32), jnp.zeros(w_second.shape, jnp.float32), store_zeros)
        _, acc_first, acc_second, grad_embedded = lax.fori_loop(0, n_ticks, bwd_tick, bwd_init)

        grad_lookup_in = lax.psum(jnp.where(is_first, grad_embedded, 0), "stage")
        seg_ids = jnp.where(tok_here, local_tok, slice_rows).reshape(-1)
        grad_lookup = jax.ops.segment_sum(grad_lookup_in.reshape(-1, model_dim).astype(jnp.float32), seg_ids, num_segments=slice_rows)
        mean_loss = (loss_sum / (micro_count * micro_tokens)).reshape(1)
        return mean_loss, acc_first[None], acc_second[None], grad_head + grad_lookup

    return jax.shard_map(
        stage_body,
        mesh=mesh,
        in_specs=(P("dp", None), P("dp", None), P("stage", None), P("stage", None, None), P("stage", None, None)),
        out_specs=(P("dp"), P(("dp", "stage"), None, None), P(("dp", "stage"), None, None), P(("dp", "stage"), None)),
        check_vma=False,
    )
```

profile of v0, /device:TPU:0, one launch (start us, length us, event | category | flops | bytes accessed | tf_op | source)
XLA Modules:
  0.0 3862.0 jit_solution(3237469902909002794)
XLA Ops:
  9.4 46.0 %gather_fusion = bf16[8192,768]{1,0:T(8,128)(2,1)} fusion(bf16[12576,768]{1,0:T(8,128)(2,1)} %param.17, s32[8192]{0:T(1024)S(1)} %broadcast_clamp_fusion), kind=kCustom, calls=%fused_computation | custom fusion | bytes 25198592 | tf_op jit(solution)/shard_map/jit(_take)/gather | solution.py:60
  66.0 217.3 %all-reduce.5.cloned.1.call-done = bf16[16,512,768]{2,1,0:T(8,128)(2,1)} async-done(((bf16[16,512,768]{2,1,0:T(8,128)(2,1)}), bf16[16,512,768]{2,1,0:T(8,128)(2,1)}) %all-reduce.5.cloned.1.call-update) | async-done | bytes 12582928 | tf_op jit(solution)/shard_map/psum | solution.py:61
  294.9 463.8 %while.53 = (s32[]{:T(128)}, bf16[512,768]{1,0:T(8,128)(2,1)S(1)}, bf16[16,512,768]{2,1,0:T(8,128)(2,1)}, bf16[16,512,768]{2,1,0:T(8,128)(2,1)}, s32[]{:T(128)},...) while((s32[]{:T(128)}, bf16[512,768]{1,0:T(8,128)(2,1)S(1)}, ...), condition=%wide.region_4.5_spmd, body=%wide.region_1.4_spmd.sunk | while | flops 4848353280 | bytes 25166612 | solution.py:76
  778.7 225.2 %all-reduce.7.cloned.1.call-done = bf16[16,512,768]{2,1,0:T(8,128)(2,1)} async-done(((bf16[16,512,768]{2,1,0:T(8,128)(2,1)}), bf16[16,512,768]{2,1,0:T(8,128)(2,1)}) %all-reduce.7.cloned.1.call-update) | async-done | bytes 12582928 | tf_op jit(solution)/shard_map/psum | solution.py:79
  1003.9 1697.4 %while.55 = (s32[]{:T(128)}, f32[12576,768]{1,0:T(8,128)}, f32[]{:T(128)}, f32[16,512,768]{2,1,0:T(8,128)}, bf16[16,512,768]{2,1,0:T(8,128)(2,1)}, /*index=5*/bf...) while((s32[]{:T(128)}, f32[12576,768]{1,0:T(8,128)}, f32[]{:T(128)}, ...), condition=%wide.region_15.16_spmd.clone, body=%wide.region_7.15_spmd.clone.sunk | while | flops 29825435648 | bytes 234713264 | solution.py:98
  1174.3 34.7 select_add_fusion.2
  1280.3 34.7 select_add_fusion.2
  1386.5 34.7 select_add_fusion.2
  1492.6 34.7 select_add_fusion.2
  1598.7 34.7 select_add_fusion.2
  1704.7 34.7 select_add_fusion.2
  1810.9 34.7 select_add_fusion.2
  1917.0 34.7 select_add_fusion.2
  2023.0 34.7 select_add_fusion.2
  2129.0 34.7 select_add_fusion.2
  2235.1 34.7 select_add_fusion.2
  2341.2 34.7 select_add_fusion.2
  2447.2 34.7 select_add_fusion.2
  2553.4 34.7 select_add_fusion.2
  2659.4 34.7 select_add_fusion.2
  2746.9 801.1 %while.54 = (s32[]{:T(128)}, bf16[512,768]{1,0:T(8,128)(2,1)S(1)}, f32[768,3072]{1,0:T(8,128)}, f32[3072,768]{1,0:T(8,128)}, bf16[16,512,768]{2,1,0:T(8,128)(2,1...) while((s32[]{:T(128)}, bf16[512,768]{1,0:T(8,128)(2,1)S(1)}, ...), condition=%wide.region_20.21_spmd, body=%wide.region_17.20_spmd.sunk | while | flops 12131893248 | bytes 246941840 | solution.py:120
  2771.3 85.6 %collective-permute-done.1 = bf16[512,768]{1,0:T(8,128)(2,1)S(1)} collective-permute-done((bf16[512,768]{1,0:T(8,128)(2,1)S(1)}, bf16[512,768]{1,0:T(8,128)(2,1)S(1)}, u32[]{:S(2)}, u32[]{:S(2)}) %collective-permute-start.1) | collective-permute-done | bytes 786464 | tf_op jit(solution)/shard_map/while/body/eval_jaxpr/ppermute | solution.py:117
  3559.4 214.5 %all-reduce.9.cloned.1.call-done = bf16[8192,768]{1,0:T(8,128)(2,1)} async-done(((bf16[8192,768]{1,0:T(8,128)(2,1)}), bf16[8192,768]{1,0:T(8,128)(2,1)}) %all-reduce.9.cloned.1.call-update) | async-done | bytes 12582928 | tf_op jit(solution)/shard_map/psum | solution.py:122
  3773.9 80.2 %scatter_custom_fusion = f32[12576,768]{1,0:T(8,128)} fusion(f32[12576,768]{1,0:T(8,128)} %get-tuple-element.537, s32[8192]{0:T(1024)S(1)} %bitcast.121, bf16[8192,768]{1,0:T(8,128)(2,1)} %all-reduce.9.cloned.1.call-done), kind=kCustom, calls=%fused_computation.88 | custom fusion | flops 12582912 | bytes 51216384 | tf_op jit(solution)/shard_map/scatter-add | solution.py:124
  (981 shorter events, 3056.7 us)
Async XLA Ops:
  7.2 276.2 %all-reduce.5.cloned.1.call-start = ((), (), s32[]{:S(2)}) async-start(), calls=%async_computation | async-start | bytes 25165824 | tf_op jit(solution)/shard_map/psum | solution.py:61
  65.5 938.4 %all-reduce.7.cloned.1.call-start = ((), (), s32[]{:S(2)}) async-start(), calls=%async_computation.1 | async-start | bytes 25165824 | tf_op jit(solution)/shard_map/psum | solution.py:79
  364.4 13.4 collective-permute-start
  520.4 13.4 collective-permute-start
  693.3 22.4 collective-permute-start
  736.2 22.4 collective-permute-start
  1004.0 103.0 %all-reduce.11.cloned.1.call-start = ((), (), s32[]{:S(2)}) async-start(), calls=%async_computation.3 | async-start | bytes 3145728 | tf_op jit(solution)/shard_map/while/body/eval_jaxpr/psum | solution.py:93
  1109.7 103.4 %all-reduce.11.cloned.1.call-start = ((), (), s32[]{:S(2)}) async-start(), calls=%async_computation.3 | async-start | bytes 3145728 | tf_op jit(solution)/shard_map/while/body/eval_jaxpr/psum | solution.py:93
  1215.7 103.4 %all-reduce.11.cloned.1.call-start = ((), (), s32[]{:S(2)}) async-start(), calls=%async_computation.3 | async-start | bytes 3145728 | tf_op jit(solution)/shard_map/while/body/eval_jaxpr/psum | solution.py:93
  1321.9 103.4 %all-reduce.11.cloned.1.call-start = ((), (), s32[]{:S(2)}) async-start(), calls=%async_computation.3 | async-start | bytes 3145728 | tf_op jit(solution)/shard_map/while/body/eval_jaxpr/psum | solution.py:93
  1428.0 103.5 %all-reduce.11.cloned.1.call-start = ((), (), s32[]{:S(2)}) async-start(), calls=%async_computation.3 | async-start | bytes 3145728 | tf_op jit(solution)/shard_map/while/body/eval_jaxpr/psum | solution.py:93
  1534.1 103.4 %all-reduce.11.cloned.1.call-start = ((), (), s32[]{:S(2)}) async-start(), calls=%async_computation.3 | async-start | bytes 3145728 | tf_op jit(solution)/shard_map/while/body/eval_jaxpr/psum | solution.py:93
  1640.1 103.4 %all-reduce.11.cloned.1.call-start = ((), (), s32[]{:S(2)}) async-start(), calls=%async_computation.3 | async-start | bytes 3145728 | tf_op jit(solution)/shard_map/while/body/eval_jaxpr/psum | solution.py:93
  1746.2 103.5 %all-reduce.11.cloned.1.call-start = ((), (), s32[]{:S(2)}) async-start(), calls=%async_computation.3 | async-start | bytes 3145728 | tf_op jit(solution)/shard_map/while/body/eval_jaxpr/psum | solution.py:93
  1852.4 103.4 %all-reduce.11.cloned.1.call-start = ((), (), s32[]{:S(2)}) async-start(), calls=%async_computation.3 | async-start | bytes 3145728 | tf_op jit(solution)/shard_map/while/body/eval_jaxpr/psum | solution.py:93
  1958.4 103.4 %all-reduce.11.cloned.1.call-start = ((), (), s32[]{:S(2)}) async-start(), calls=%async_computation.3 | async-start | bytes 3145728 | tf_op jit(solution)/shard_map/while/body/eval_jaxpr/psum | solution.py:93
  2064.4 103.4 %all-reduce.11.cloned.1.call-start = ((), (), s32[]{:S(2)}) async-start(), calls=%async_computation.3 | async-start | bytes 3145728 | tf_op jit(solution)/shard_map/while/body/eval_jaxpr/psum | solution.py:93
  2170.5 103.4 %all-reduce.11.cloned.1.call-start = ((), (), s32[]{:S(2)}) async-start(), calls=%async_computation.3 | async-start | bytes 3145728 | tf_op jit(solution)/shard_map/while/body/eval_jaxpr/psum | solution.py:93
  2276.6 103.4 %all-reduce.11.cloned.1.call-start = ((), (), s32[]{:S(2)}) async-start(), calls=%async_computation.3 | async-start | bytes 3145728 | tf_op jit(solution)/shard_map/while/body/eval_jaxpr/psum | solution.py:93
  2382.6 103.4 %all-reduce.11.cloned.1.call-start = ((), (), s32[]{:S(2)}) async-start(), calls=%async_computation.3 | async-start | bytes 3145728 | tf_op jit(solution)/shard_map/while/body/eval_jaxpr/psum | solution.py:93
  2488.7 103.5 %all-reduce.11.cloned.1.call-start = ((), (), s32[]{:S(2)}) async-start(), calls=%async_computation.3 | async-start | bytes 3145728 | tf_op jit(solution)/shard_map/while/body/eval_jaxpr/psum | solution.py:93
  2594.8 103.4 %all-reduce.11.cloned.1.call-start = ((), (), s32[]{:S(2)}) async-start(), calls=%async_computation.3 | async-start | bytes 3145728 | tf_op jit(solution)/shard_map/while/body/eval_jaxpr/psum | solution.py:93
  2701.3 1072.6 %all-reduce.9.cloned.1.call-start = ((), (), s32[]{:S(2)}) async-start(), calls=%async_computation.2 | async-start | bytes 25165824 | tf_op jit(solution)/shard_map/psum | solution.py:122
  2767.7 89.2 %collective-permute-start.1 = (bf16[512,768]{1,0:T(8,128)(2,1)S(1)}, bf16[512,768]{1,0:T(8,128)(2,1)S(1)}, u32[]{:S(2)}, u32[]{:S(2)}) collective-permute-start(bf16[512,768]{1,0:T(8,128)(2,1)S(1)} %get-tuple-element.804), channel_id=1, source_target_pairs={{1,0},{2,1},{3,2},{5,4},{6,5},{7,6}} | collective-permute-start | bytes 2359304 | tf_op jit(solution)/shard_map/while/body/eval_jaxpr/ppermute | solution.py:117
  (200 other events, 1146.2 us)
Sparse Core Ops, SparseCore 0:
  65.6 217.6 all-reduce.4
  778.1 225.7 all-reduce.6
  1069.1 37.8 all-reduce.10
  1174.4 38.6 all-reduce.10
  1280.4 38.6 all-reduce.10
  1386.6 38.6 all-reduce.10
  1492.7 38.6 all-reduce.10
  1598.8 38.6 all-reduce.10
  1704.9 38.6 all-reduce.10
  1811.0 38.6 all-reduce.10
  1917.1 38.6 all-reduce.10
  2023.1 38.6 all-reduce.10
  2129.2 38.6 all-reduce.10
  2235.2 38.6 all-reduce.10
  2341.3 38.6 all-reduce.10
  2447.3 38.6 all-reduce.10
  2553.5 38.6 all-reduce.10
  2659.5 38.6 all-reduce.10
  3558.8 215.0 all-reduce.8
where the time goes:
time: 3870 us; the launch traced here: 3860 us
  matrix products  1740 us (45%)
  waiting for transfers between devices  952 us (25%)
  other arithmetic  461 us (12%)
  local copies, waits for them, and re-layouts  264 us (7%)
  starting transfers between devices  231 us (6%)
  blocking collectives  183 us (5%)
    dot_general x16, matrix products, head_step(): jnp.einsum('tv,td->vd', grad_logits, normed_mb, preferred_element_type=jn...  546 us
    dot_general x16, matrix products, head_step(): jnp.einsum('tv,vd->td', grad_logits, emb_rows, preferred_element_type=jnp...  358 us
    dot_general x16, matrix products, head_step(): jnp.einsum('td,vd->tv', normed_mb, emb_rows, preferred_element_type=jnp.f...  304 us
    ppermute x19, waiting for transfers between devices, bwd_tick(): lax.ppermute(grad_in, 'stage', bwd_pairs)  242 us
    psum x1, waiting for transfers between devices, stage_body(): lax.psum(jnp.where(is_last, normed_f.astype(jnp.bfloat16), 0), 'stage')  225 us
    psum x1, waiting for transfers between devices, stage_body(): embedded = lax.psum(jnp.where(tok_here[..., None], looked_up, 0), 'stage')  217 us
    psum x1, waiting for transfers between devices, stage_body(): grad_lookup_in = lax.psum(jnp.where(is_first, grad_embedded, 0), 'stage')  214 us
    ppermute x19, starting transfers between devices, fwd_tick(): return (lax.ppermute(act_out, 'stage', fwd_pairs), saved_in, last_out)  206 us
  transfers between devices with their start and end apart: 57, of which 38 were waited for; matrix products, arithmetic and copies ran while one was open for 17% of the time, Pallas kernels for 0%

commit v1 on v0

v1 whole, which is shorter than its diff:
```python
import functools
import jax
import jax.numpy as jnp
from jax import lax
from jax.experimental import pallas as pl
from jax.experimental.pallas import tpu as pltpu
from jax.sharding import PartitionSpec as P

NORM_EPS = 1e-6
LOG2E = 1.4426950408889634
LN2 = 0.6931471805599453
GELU_K = 0.7978845608028654
GELU_A = 0.044715
SUB = 256
SUBS = 10
TILE = SUB * SUBS
GROUPS = 4
PARTS = 4
V_TILE = 640
VMEM_CAP = 56 * 1024 * 1024
BF = jnp.bfloat16
F32 = jnp.float32
NT = (((1,), (1,)), ((), ()))


def norm_f32(act_rows):
    acts_f = act_rows.astype(F32)
    return acts_f * lax.rsqrt(jnp.mean(acts_f * acts_f, axis=-1, keepdims=True) + NORM_EPS)


def alloc(*shapes):
    return pl.pallas_call(
        lambda *refs: None,
        out_specs=[pl.BlockSpec(memory_space=pl.ANY)] * len(shapes),
        out_shape=[jax.ShapeDtypeStruct(s, BF) for s in shapes],
        name="alloc",
    )()


def layer_forward_body(flags, moved_ref, here_ref, far_ref, w1_ref, w2_ref, _a, _b, _c, out_ref, save_ref, last_ref, n_ref, acc_ref):
    step = pl.program_id(0)

    @pl.when(flags[1] == 1)
    def _():
        @pl.when((step == 0) & (flags[2] == 1))
        def _():
            save_ref[0] = here_ref[0] + far_ref[...]

        @pl.when((step == 0) & (flags[2] == 0))
        def _():
            save_ref[0] = moved_ref[...]

        x = save_ref[0]
        width = w1_ref.shape[1] // PARTS
        total = None
        for part in range(PARTS):
            cols = slice(part * width, (part + 1) * width)
            pre = jnp.dot(x, w1_ref[:, cols], preferred_element_type=F32)
            inner = jnp.tanh(pre * (GELU_K + (GELU_K * GELU_A) * (pre * pre)))
            half = 0.5 * pre
            hidden = (half + half * inner).astype(BF)
            term = jnp.dot(hidden, w2_ref[cols, :], preferred_element_type=F32)
            total = term if total is None else total + term

        @pl.when(step == 0)
        def _():
            acc_ref[...] = total

        @pl.when(step > 0)
        def _():
            acc_ref[...] += total

        @pl.when(step == pl.num_programs(0) - 1)
        def _():
            out = (x.astype(F32) + acc_ref[...]).astype(BF)
            out_ref[...] = out
            last_ref[0] = out
            n_ref[0] = norm_f32(out).astype(BF)


def layer_forward(flags, moved, chip_rows, far, w1, w2, saved_in, last_out, normed, f_tile=1024):
    rows, dim = moved.shape
    ffn = w1.shape[1]
    any_spec = pl.BlockSpec(memory_space=pl.ANY)
    flat = pl.BlockSpec((rows, dim), lambda f, fl: (0, 0))
    slot = pl.BlockSpec((1, rows, dim), lambda f, fl: (fl[0], 0, 0))
    grid_spec = pltpu.PrefetchScalarGridSpec(
        num_scalar_prefetch=1,
        grid=(ffn // f_tile,),
        in_specs=[
            flat,
            pl.BlockSpec((1, rows, dim), lambda f, fl: (fl[3], 0, 0)),
            flat,
            pl.BlockSpec((dim, f_tile), lambda f, fl: (0, f * fl[1])),
            pl.BlockSpec((f_tile, dim), lambda f, fl: (f * fl[1], 0)),
            any_spec, any_spec, any_spec,
        ],
        out_specs=[flat, slot, slot, slot],
        scratch_shapes=[pltpu.VMEM((rows, dim), F32)],
    )
    return pl.pallas_call(
        layer_forward_body,
        grid_spec=grid_spec,
        out_shape=[jax.ShapeDtypeStruct((rows, dim), BF)] + [jax.ShapeDtypeStruct(saved_in.shape, BF)] * 3,
        input_output_aliases={6: 1, 7: 2, 8: 3},
        compiler_params=pltpu.CompilerParams(vmem_limit_bytes=VMEM_CAP),
        cost_estimate=pl.CostEstimate(flops=4 * rows * dim * ffn, bytes_accessed=4 * dim * ffn, transcendentals=rows * ffn),
        name="layer_fwd",
    )(flags, moved, chip_rows, far, w1, w2, saved_in, last_out, normed)


def head_forward_body(n_valid, log_scale, n_ref, e_ref, lab_ref, p_ref, m_ref, st_ref, run):
    tile, chunk = pl.program_id(0), pl.program_id(1)

    @pl.when(tile == 0)
    def _():
        run[chunk, 0:1, :] = jnp.full((1, run.shape[2]), -jnp.inf, F32)
        run[chunk, 1:3, :] = jnp.zeros((2, run.shape[2]), F32)

    n_rows = n_ref[0]
    lab = lab_ref[0] - tile * TILE
    top, tot, hit = run[chunk, 0:1, :], run[chunk, 1:2, :], run[chunk, 2:3, :]
    rows = lax.broadcasted_iota(jnp.int32, (SUB, n_rows.shape[0]), 0)
    for sub in range(SUBS):
        cut = slice(sub * SUB, (sub + 1) * SUB)
        logit = lax.dot_general(e_ref[cut, :], n_rows, NT, preferred_element_type=F32) * log_scale
        if sub == SUBS - 1:
            logit = jnp.where(rows < n_valid - tile * TILE - sub * SUB, logit, -jnp.inf)
        hit = hit + jnp.sum(jnp.where(rows == lab - sub * SUB, logit, 0.0), axis=0, keepdims=True)
        new_top = jnp.maximum(top, jnp.max(logit, axis=0, keepdims=True))
        expo = jnp.exp2(logit - new_top)
        tot = tot * jnp.exp2(top - new_top) + jnp.sum(expo, axis=0, keepdims=True)
        p_ref[0, cut, :] = expo.astype(BF)
        m_ref[0, 0, sub:sub + 1, :] = new_top
        top = new_top
    run[chunk, 0:1, :] = top
    run[chunk, 1:2, :] = tot
    run[chunk, 2:3, :] = hit
    st_ref[0, 0:1, :] = top
    st_ref[0, 1:2, :] = tot
    st_ref[0, 2:3, :] = hit


def head_forward(normed, emb_pad, labels, n_valid, log_scale):
    chunks, rows, dim = normed.shape
    padded = emb_pad.shape[0]
    tiles = padded // TILE
    row = pl.BlockSpec((1, 1, rows), lambda t, c: (c, 0, 0))
    return pl.pallas_call(
        functools.partial(head_forward_body, n_valid, log_scale),
        grid=(tiles, chunks),
        in_specs=[
            pl.BlockSpec((1, rows, dim), lambda t, c: (c, 0, 0)),
            pl.BlockSpec((TILE, dim), lambda t, c: (t, 0)),
            row,
        ],
        out_specs=[
            pl.BlockSpec((1, TILE, rows), lambda t, c: (c, t, 0)),
            pl.BlockSpec((1, 1, SUBS, rows), lambda t, c: (c, t, 0, 0)),
            pl.BlockSpec((1, 3, rows), lambda t, c: (c, 0, 0)),
        ],
        out_shape=[
            jax.ShapeDtypeStruct((chunks, padded, rows), BF),
            jax.ShapeDtypeStruct((chunks, tiles, SUBS, rows), F32),
            jax.ShapeDtypeStruct((chunks, 3, rows), F32),
        ],
        scratch_shapes=[pltpu.VMEM((chunks, 3, rows), F32)],
        compiler_params=pltpu.CompilerParams(vmem_limit_bytes=VMEM_CAP),
        cost_estimate=pl.CostEstimate(flops=2 * chunks * rows * dim * padded, bytes_accessed=padded * (2 * dim + 2 * rows * chunks), transcendentals=rows * chunks * padded),
        name="head_fwd",
    )(normed, emb_pad, labels)


def head_backward_body(p_ref, c_ref, lab_ref, g_ref, et_ref, d_ref, out_ref, acc_ref):
    tile, chunk = pl.program_id(0), pl.program_id(1)
    lab = lab_ref[0] - tile * TILE
    gain = g_ref[0]
    rows = lax.broadcasted_iota(jnp.int32, (SUB, lab.shape[1]), 0)
    total = None
    for sub in range(SUBS):
        cut = slice(sub * SUB, (sub + 1) * SUB)
        prob = p_ref[0, cut, :].astype(F32) * c_ref[0, 0, sub:sub + 1, :]
        delta = jnp.where(rows == lab - sub * SUB, gain, prob).astype(BF)
        d_ref[0, cut, :] = delta
        term = jnp.dot(et_ref[:, cut], delta, preferred_element_type=F32)
        total = term if total is None else total + term

    @pl.when(tile == 0)
    def _():
        acc_ref[chunk] = total

    @pl.when(tile > 0)
    def _():
        acc_ref[chunk] += total

    @pl.when(tile == pl.num_programs(0) - 1)
    def _():
        out_ref[0] = acc_ref[chunk].T.astype(BF)


def head_backward(expo, coef, labels, gain, emb_t):
    chunks, padded, rows = expo.shape
    dim = emb_t.shape[0]
    tiles = padded // TILE
    row = pl.BlockSpec((1, 1, rows), lambda t, c: (c, 0, 0))
    block = pl.BlockSpec((1, TILE, rows), lambda t, c: (c, t, 0))
    end = tiles - 1
    return pl.pallas_call(
        head_backward_body,
        grid=(tiles, chunks),
        in_specs=[
            block,
            pl.BlockSpec((1, 1, SUBS, rows), lambda t, c: (c, t, 0, 0)),
            row,
            row,
            pl.BlockSpec((dim, TILE), lambda t, c: (0, t)),
        ],
        out_specs=[block, pl.BlockSpec((1, rows, dim), lambda t, c: (c * (t // end), 0, 0))],
        out_shape=[jax.ShapeDtypeStruct(expo.shape, BF), jax.ShapeDtypeStruct((chunks, rows, dim), BF)],
        scratch_shapes=[pltpu.VMEM((chunks, dim, rows), F32)],
        input_output_aliases={0: 0},
        compiler_params=pltpu.CompilerParams(vmem_limit_bytes=VMEM_CAP),
        cost_estimate=pl.CostEstimate(flops=2 * chunks * rows * dim * padded, bytes_accessed=padded * (2 * dim + 4 * rows * chunks), transcendentals=0),
        name="head_bwd",
    )(expo, coef, labels, gain, emb_t)


def table_grad_body(groups, *refs):
    deltas, normed, out_ref = refs[:groups], refs[groups:2 * groups], refs[2 * groups]
    total = None
    for d_ref, n_ref in zip(deltas, normed):
        for chunk in range(d_ref.shape[0]):
            term = jnp.dot(d_ref[chunk], n_ref[chunk], preferred_element_type=F32)
            total = term if total is None else total + term
    out_ref[...] = total


def table_grad(deltas, normed, slice_rows, v_tile):
    chunks, rows, dim = normed[0].shape
    groups = len(deltas)
    tokens = groups * chunks * rows
    return pl.pallas_call(
        functools.partial(table_grad_body, groups),
        grid=(-(-slice_rows // v_tile),),
        in_specs=[pl.BlockSpec((chunks, v_tile, rows), lambda v: (0, v, 0))] * groups
        + [pl.BlockSpec((chunks, rows, dim), lambda v: (0, 0, 0), pipeline_mode=pl.Buffered(1))] * groups,
        out_specs=pl.BlockSpec((v_tile, dim), lambda v: (v, 0)),
        out_shape=jax.ShapeDtypeStruct((slice_rows, dim), F32),
        compiler_params=pltpu.CompilerParams(vmem_limit_bytes=VMEM_CAP),
        cost_estimate=pl.CostEstimate(flops=2 * slice_rows * dim * tokens, bytes_accessed=2 * slice_rows * tokens, transcendentals=0),
        name="table_grad",
    )(*deltas, *normed)


def layer_backward_body(flags, x_ref, moved_ref, top_ref, mdx_ref, w1_ref, w2_ref, _a, _b, _c, _d, gin_ref, g_ref, h_ref, gp_ref, dx_ref, acc_ref):
    step = pl.program_id(0)
    end = pl.num_programs(0) - 1

    @pl.when((step == end) & (flags[4] == 0))
    def _():
        dx_ref[0] = mdx_ref[...]

    @pl.when(flags[1] == 1)
    def _():
        @pl.when((step == 0) & (flags[2] == 1))
        def _():
            g_ref[0] = top_ref[0]

        @pl.when((step == 0) & (flags[2] == 0))
        def _():
            g_ref[0] = moved_ref[...]

        x = x_ref[0]
        grad_out = g_ref[0]
        width = w1_ref.shape[1] // PARTS
        total = None
        for part in range(PARTS):
            cols = slice(part * width, (part + 1) * width)
            pre = jnp.dot(x, w1_ref[:, cols], preferred_element_type=F32)
            grad_hidden = lax.dot_general(grad_out, w2_ref[cols, :], NT, preferred_element_type=F32)
            sq = pre * pre
            inner = jnp.tanh(pre * (GELU_K + (GELU_K * GELU_A) * sq))
            side = 0.5 + 0.5 * inner
            bend = (0.5 - 0.5 * inner * inner) * (GELU_K + (3.0 * GELU_K * GELU_A) * sq)
            h_ref[0, :, cols] = (pre * side).astype(BF)
            grad_pre = (grad_hidden * (side + pre * bend)).astype(BF)
            gp_ref[0, :, cols] = grad_pre
            term = lax.dot_general(grad_pre, w1_ref[:, cols], NT, preferred_element_type=F32)
            total = term if total is None else total + term

        @pl.when(step == 0)
        def _():
            acc_ref[...] = total

        @pl.when(step > 0)
        def _():
            acc_ref[...] += total

        @pl.when(step == end)
        def _():
            grad_in = (grad_out.astype(F32) + acc_ref[...]).astype(BF)
            gin_ref[...] = grad_in

            @pl.when(flags[4] == 1)
            def _():
                dx_ref[0] = grad_in


def layer_backward(flags, saved_in, moved, grad_last, moved_dx, w1, w2, grads, hidden, grad_pre, dx_all, f_tile=768):
    rows, dim = moved.shape
    ffn = w1.shape[1]
    any_spec = pl.BlockSpec(memory_space=pl.ANY)
    wide = pl.BlockSpec((1, rows, f_tile), lambda f, fl: (fl[0], 0, f * fl[1]))
    flat = pl.BlockSpec((rows, dim), lambda f, fl: (0, 0))
    slot = pl.BlockSpec((1, rows, dim), lambda f, fl: (fl[0], 0, 0))
    grid_spec = pltpu.PrefetchScalarGridSpec(
        num_scalar_prefetch=1,
        grid=(ffn // f_tile,),
        in_specs=[
            slot,
            flat,
            pl.BlockSpec((1, rows, dim), lambda f, fl: (fl[3], 0, 0)),
            flat,
            pl.BlockSpec((dim, f_tile), lambda f, fl: (0, f * fl[1])),
            pl.BlockSpec((f_tile, dim), lambda f, fl: (f * fl[1], 0)),
            any_spec, any_spec, any_spec, any_spec,
        ],
        out_specs=[flat, slot, wide, wide, pl.BlockSpec((1, rows, dim), lambda f, fl: (fl[5], 0, 0))],
        scratch_shapes=[pltpu.VMEM((rows, dim), F32)],
    )
    return pl.pallas_call(
        layer_backward_body,
        grid_spec=grid_spec,
        out_shape=[jax.ShapeDtypeStruct((rows, dim), BF)] + [jax.ShapeDtypeStruct(a.shape, BF) for a in (grads, hidden, grad_pre, dx_all)],
        input_output_aliases={7: 1, 8: 2, 9: 3, 10: 4},
        compiler_params=pltpu.CompilerParams(vmem_limit_bytes=VMEM_CAP),
        cost_estimate=pl.CostEstimate(flops=6 * rows * dim * ffn, bytes_accessed=4 * dim * ffn + 4 * rows * ffn, transcendentals=rows * ffn),
        name="layer_bwd",
    )(flags, saved_in, moved, grad_last, moved_dx, w1, w2, grads, hidden, grad_pre, dx_all)


def take(store, slot):
    return lax.dynamic_index_in_dim(store, slot, 0, keepdims=False)


def solution(mesh):
    n_stage = mesh.shape["stage"]
    last = n_stage - 1
    fwd_pairs = [(src, src + 1) for src in range(last)]
    bwd_pairs = [(src + 1, src) for src in range(last)]

    def stage_body(token_ids, label_ids, emb_rows, w_in, w_out):
        stage = lax.axis_index("stage")
        is_first = (stage == 0).astype(jnp.int32)
        is_last = (stage == last).astype(jnp.int32)
        micro_count, micro_tokens = token_ids.shape
        slice_rows, dim = emb_rows.shape
        ffn = w_in.shape[2]
        scale = dim ** -0.5
        w1, w2 = w_in[0], w_out[0]
        row_start = stage * slice_rows
        padded = -(-slice_rows // TILE) * TILE
        spare = micro_count
        per = micro_count // GROUPS

        def hop(value, *pairs):
            return lax.ppermute(value, "stage", pairs)

        def place(idx):
            active = (idx >= 0) & (idx < micro_count)
            return jnp.where(active, idx, spare), active.astype(jnp.int32), jnp.clip(idx, 0, micro_count - 1)

        local_tok = token_ids - row_start
        tok_here = (local_tok >= 0) & (local_tok < slice_rows)
        looked_up = jnp.take(emb_rows, jnp.clip(local_tok, 0, slice_rows - 1), axis=0)
        own_rows = jnp.where(tok_here[..., None], looked_up, 0)
        chip_rows = own_rows + hop(own_rows, (1, 0), (3, 2))

        emb_pad = jnp.pad(emb_rows, ((0, padded - slice_rows), (0, 0)))
        emb_t = emb_pad.T
        local_lab = label_ids - row_start
        labels = jnp.where((local_lab >= 0) & (local_lab < slice_rows), local_lab, -1)[:, None]

        act_zero = jnp.zeros((micro_tokens, dim), BF)
        store = (micro_count + 1, micro_tokens, dim)
        wide = (micro_count + 1, micro_tokens, ffn)
        saved_in, last_out, normed, grads, dx_all, hidden, grad_pre = alloc(store, store, store, store, store, wide, wide)

        def far_rows(idx):
            return hop(take(chip_rows, jnp.minimum(idx, micro_count - 1)), (2, 0))

        def fwd_tick(tick, carry):
            moved, far, out, saved_in, last_out, normed = carry
            next_moved = lax.ppermute(out, "stage", fwd_pairs)
            next_far = far_rows(tick + 1)
            slot, active, idx = place(tick - 2 * stage)
            flags = jnp.stack([slot, active, is_first, idx])
            out, saved_in, last_out, normed = layer_forward(flags, moved, chip_rows, far, w1, w2, saved_in, last_out, normed)
            return next_moved, next_far, out, saved_in, last_out, normed

        carry = (act_zero, far_rows(0), act_zero, saved_in, last_out, normed)
        carry = lax.fori_loop(0, micro_count + 2 * last, fwd_tick, carry)
        _, _, _, saved_in, last_out, normed = carry

        cuts = [slice(g * per, (g + 1) * per) for g in range(GROUPS)]
        n_parts, expo, maxes, stats = [], [], [], []
        for cut in cuts:
            own = normed[cut]
            near = hop(own, (3, 2))
            cross = hop(own, (3, 1))
            final = hop(cross, (1, 0))
            part = jnp.where(stage == 3, own, jnp.where(stage == 2, near, jnp.where(stage == 1, cross, final)))
            n_parts.append(part)
            res = head_forward(part, emb_pad, labels[cut], slice_rows, scale * LOG2E)
            expo.append(res[0])
            maxes.append(res[1])
            stats.append(res[2])

        every = lax.all_gather(jnp.concatenate(stats), "stage")
        top = jnp.max(every[:, :, 0], axis=0)
        denom = jnp.sum(every[:, :, 1] * jnp.exp2(every[:, :, 0] - top), axis=0)
        hit = jnp.sum(every[:, :, 2], axis=0)
        mean_loss = (jnp.sum(jnp.log2(denom) + top - hit) * (LN2 / (micro_count * micro_tokens))).reshape(1)
        ratio = scale / denom
        gain = ((jnp.exp2(hit - top) / denom - 1.0) * scale)[:, None]

        deltas, grad_last = [], []
        for g, cut in enumerate(cuts):
            coef = jnp.exp2(maxes[g] - top[cut, None, None]) * ratio[cut, None, None]
            delta, part = head_backward(expo[g], coef, labels[cut], gain[cut], emb_t)
            deltas.append(delta)
            near = hop(part, (0, 1), (2, 3)).astype(F32)
            pair = part.astype(F32) + near
            far = hop(pair.astype(BF), (1, 3)).astype(F32)
            _, pull = jax.vjp(norm_f32, last_out[cut])
            grad_last.append(pull(pair + far)[0])
        grad_last = jnp.concatenate(grad_last)

        grad_head = table_grad(deltas, n_parts, slice_rows, V_TILE)

        def bwd_tick(tick, carry):
            moved, moved_dx, grad_in, grads, hidden, grad_pre, dx_all = carry
            next_moved = lax.ppermute(grad_in, "stage", bwd_pairs)
            next_dx = hop(grad_in, (0, 2))
            slot, active, idx = place(tick - 2 * (last - stage))
            dx_slot, _, _ = place(tick - 2 * last - 2 + 2 * is_first)
            flags = jnp.stack([slot, active, is_last, idx, is_first, dx_slot])
            grad_in, grads, hidden, grad_pre, dx_all = layer_backward(
                flags, saved_in, moved, grad_last, moved_dx, w1, w2, grads, hidden, grad_pre, dx_all)
            return next_moved, next_dx, grad_in, grads, hidden, grad_pre, dx_all

        carry = (act_zero, act_zero, act_zero, grads, hidden, grad_pre, dx_all)
        carry = lax.fori_loop(0, micro_count + 2 * last + 2, bwd_tick, carry)
        _, _, _, grads, hidden, grad_pre, dx_all = carry

        def clear(value):
            blank = jnp.zeros((1,) + value.shape[1:], BF)
            return lax.dynamic_update_slice(value, blank, (spare, 0, 0)).reshape(-1, value.shape[2])

        grad_first = jnp.einsum("td,tf->df", clear(saved_in), clear(grad_pre), preferred_element_type=F32)
        grad_second = jnp.einsum("tf,td->fd", clear(hidden), clear(grads), preferred_element_type=F32)
        dx_rows = dx_all[:micro_count]
        dx_rows = jnp.where(stage % 2 == 0, dx_rows, hop(dx_rows, (0, 1), (2, 3)))
        seg = jnp.where(tok_here, local_tok, slice_rows).reshape(-1)
        grad_emb = grad_head.at[seg].add(dx_rows.reshape(-1, dim).astype(F32), mode="drop")
        return mean_loss, grad_first[None], grad_second[None], grad_emb

    return jax.shard_map(
        stage_body,
        mesh=mesh,
        in_specs=(P("dp", None), P("dp", None), P("stage", None), P("stage", None, None), P("stage", None, None)),
        out_specs=(P("dp"), P(("dp", "stage"), None, None), P(("dp", "stage"), None, None), P(("dp", "stage"), None)),
        check_vma=False,
    )
```

time: 3870 us -> 2540 us (0.66)
  matrix products: 1740 us -> 99.2 us
  Pallas kernels: 0 us -> 1290 us
  waiting for transfers between devices: 952 us -> 225 us
  other arithmetic: 461 us -> 202 us
  blocking collectives: 183 us -> 19.6 us
  starting transfers between devices: 231 us -> 363 us
  local copies, waits for them, and re-layouts: 264 us -> 321 us
    dot_general x144 -> x2, matrix products: 1740 us -> 99.2 us  [the longest x1 52 us: stage_body(): jnp.einsum('tf,td->fd', clear(hidden), clear(grads), preferred_element_ty...]
    pallas_call x0 -> x56, Pallas kernels: none -> 1290 us  [the longest x24 355 us: layer_backward(): pl.pallas_call(layer_backward_body, grid_spec=grid_spec, out_shape=[jax.S...]
    psum x19 -> x0, waiting for transfers between devices: 710 us -> none  [the longest x1 225 us: stage_body(): lax.psum(jnp.where(is_last, normed_f.astype(jnp.bfloat16), 0), 'stage')]
    reduce_sum x33 -> x1, other arithmetic: 214 us -> 0.04 us  [stage_body(): denom = jnp.sum(every[:, :, 1] * jnp.exp2(every[:, :, 0] - top), axis=0)]
    ppermute x38 -> x115, starting transfers between devices: 231 us -> 363 us  [the longest x69 230 us: hop(): return lax.ppermute(value, 'stage', pairs)]
    while x0 -> x92, local copies, waits for them, and re-layouts: none -> 105 us
    pmax x16 -> x0, blocking collectives: 91.9 us -> none  [head_step(): row_max = lax.pmax(jnp.max(logits, axis=1), 'stage')]
    psum x16 -> x0, blocking collectives: 90.7 us -> none  [head_step(): lax.psum(jnp.stack([jnp.sum(exp_logits, axis=1), jnp.sum(jnp.where(is_lab...]
  transfers between devices with their start and end apart: 57 -> 115, of which waited for: 38 -> 18; matrix products, arithmetic and copies ran while one was open for 17% -> 12% of each run, Pallas kernels for 0% -> 41%
where the time goes in v1:
time: 2540 us; the launch traced here: 2520 us
  Pallas kernels  1290 us (51%)
  starting transfers between devices  363 us (14%)
  local copies, waits for them, and re-layouts  321 us (13%)
  waiting for transfers between devices  225 us (9%)
  other arithmetic  202 us (8%)
  matrix products  99.2 us (4%)
    pallas_call x24, Pallas kernels, layer_backward(): pl.pallas_call(layer_backward_body, grid_spec=grid_spec, out_shape=[jax.S...  355 us
    pallas_call x4, Pallas kernels, head_forward(): pl.pallas_call(functools.partial(head_forward_body, n_valid, log_scale),...  266 us
    pallas_call x4, Pallas kernels, head_backward(): pl.pallas_call(head_backward_body, grid=(tiles, chunks), in_specs=[block,...  261 us
    ppermute x69, starting transfers between devices, hop(): return lax.ppermute(value, 'stage', pairs)  230 us
    pallas_call x22, Pallas kernels, layer_forward(): pl.pallas_call(layer_forward_body, grid_spec=grid_spec, out_shape=[jax.Sh...  229 us
    pallas_call x1, Pallas kernels, table_grad(): pl.pallas_call(functools.partial(table_grad_body, groups), grid=(-(-slice...  177 us
    ppermute x69, waiting for transfers between devices, hop(): return lax.ppermute(value, 'stage', pairs)  121 us
    while x92, local copies, waits for them, and re-layouts  105 us
  transfers between devices with their start and end apart: 115, of which 18 were waited for; matrix products, arithmetic and copies ran while one was open for 12% of the time, Pallas kernels for 41%

profile of v1, /device:TPU:0, one launch (start us, length us, event | category | flops | bytes accessed | tf_op | source)
XLA Modules:
  0.0 2521.0 jit_solution(2077968816160281896)
XLA Ops:
  2.8 46.0 %gather_fusion = bf16[8192,768]{1,0:T(8,128)(2,1)} fusion(bf16[12576,768]{1,0:T(8,128)(2,1)} %param.11, s32[8192]{0:T(1024)S(1)} %broadcast_clamp_fusion), kind=kCustom, calls=%fused_computation | custom fusion | bytes 25198592 | tf_op jit(solution)/shard_map/jit(_take)/gather | solution.py:375
  100.4 491.5 %while.54 = (s32[]{:T(128)}, bf16[512,768]{1,0:T(8,128)(2,1)S(1)}, bf16[512,768]{1,0:T(8,128)(2,1)S(1)}, bf16[512,768]{1,0:T(8,128)(2,1)S(1)}, bf16[17,512,768]{...) while((s32[]{:T(128)}, bf16[512,768]{1,0:T(8,128)(2,1)S(1)}, ...), condition=%wide.region_1.2_spmd, body=%wide.region_0.1_spmd.sunk | while | flops 4831838208 | bytes 22020488 | solution.py:402
  600.0 40.0 %collective-permute-done.8 = bf16[4,512,768]{2,1,0:T(8,128)(2,1)} collective-permute-done((bf16[4,512,768]{2,1,0:T(8,128)(2,1)}, bf16[4,512,768]{2,1,0:T(8,128)(2,1)}, u32[]{:S(2)}, u32[]{:S(2)}) %collective-permute-start.8) | collective-permute-done | bytes 3145760 | tf_op jit(solution)/shard_map/ppermute | solution.py:367
  659.0 23.8 copy.37
  685.2 25.9 %copy.58 = bf16[12576,768]{1,0:T(8,128)(2,1)} copy(bf16[12576,768]{0,1:T(8,128)(2,1)} %copy.37) | data formatting | bytes 38633472
  746.7 66.6 %head_fwd.4 = (bf16[4,12800,512]{2,1,0:T(8,128)(2,1)}, f32[4,5,10,512]{3,2,1,0:T(8,128)}, f32[4,3,512]{2,1,0:T(4,128)}) custom-call(bf16[4,512,768]{2,1,0:T(8,128)(2,1)} %get-tuple-element.909.n_ref.refs_4_, bf16[12800,768]{1,0:T(8,128)(2,1)} %pad.4.clone.e_ref, s32[4,1,512]{2,1,0:T(1,128)} %copy.39.lab_ref), custom_call_target="tpu_custom_call" | custom-call | flops 40265318400 | bytes 72089600 | tf_op jit(solution)/shard_map/head_fwd/pallas_call | solution.py:149
  824.2 66.5 %head_fwd.5 = (bf16[4,12800,512]{2,1,0:T(8,128)(2,1)}, f32[4,5,10,512]{3,2,1,0:T(8,128)}, f32[4,3,512]{2,1,0:T(4,128)}) custom-call(bf16[4,512,768]{2,1,0:T(8,128)(2,1)} %get-tuple-element.913.n_ref.refs_5_, bf16[12800,768]{1,0:T(8,128)(2,1)} %pad.4.clone.e_ref, s32[4,1,512]{2,1,0:T(1,128)} %copy.41.lab_ref), custom_call_target="tpu_custom_call" | custom-call | flops 40265318400 | bytes 72089600 | tf_op jit(solution)/shard_map/head_fwd/pallas_call | solution.py:149
  890.7 66.5 %head_fwd.6 = (bf16[4,12800,512]{2,1,0:T(8,128)(2,1)}, f32[4,5,10,512]{3,2,1,0:T(8,128)}, f32[4,3,512]{2,1,0:T(4,128)}) custom-call(bf16[4,512,768]{2,1,0:T(8,128)(2,1)} %get-tuple-element.914.n_ref.refs_6_, bf16[12800,768]{1,0:T(8,128)(2,1)} %pad.4.clone.e_ref, s32[4,1,512]{2,1,0:T(1,128)} %copy.43.lab_ref), custom_call_target="tpu_custom_call" | custom-call | flops 40265318400 | bytes 72089600 | tf_op jit(solution)/shard_map/head_fwd/pallas_call | solution.py:149
  957.2 66.7 %head_fwd.7 = (bf16[4,12800,512]{2,1,0:T(8,128)(2,1)}, f32[4,5,10,512]{3,2,1,0:T(8,128)}, f32[4,3,512]{2,1,0:T(4,128)}) custom-call(bf16[4,512,768]{2,1,0:T(8,128)(2,1)} %get-tuple-element.915.n_ref.refs_7_, bf16[12800,768]{1,0:T(8,128)(2,1)} %pad.4.clone.e_ref, s32[4,1,512]{2,1,0:T(1,128)} %slice.125.lab_ref), custom_call_target="tpu_custom_call" | custom-call | flops 40265318400 | bytes 72089600 | tf_op jit(solution)/shard_map/head_fwd/pallas_call | solution.py:149
  1049.5 65.1 %head_bwd.7 = (bf16[4,12800,512]{2,1,0:T(8,128)(2,1)}, bf16[4,512,768]{2,1,0:T(8,128)(2,1)}) custom-call(bf16[4,12800,512]{2,1,0:T(8,128)(2,1)} %get-tuple-element.829.p_ref, f32[4,5,10,512]{3,2,1,0:T(8,128)} %exponential_multiply_fusion.c_ref, s32[4,1,512]{2,1,0:T(1,128)} %slice.125.lab_ref, ...), custom_call_target="tpu_custom_call", output_to_operand_aliasing={{0}: (0, {})} | custom-call | flops 40265318400 | bytes 124518400 | tf_op jit(solution)/shard_map/head_bwd/pallas_call | solution.py:208
  1117.0 65.1 %head_bwd.6 = (bf16[4,12800,512]{2,1,0:T(8,128)(2,1)}, bf16[4,512,768]{2,1,0:T(8,128)(2,1)}) custom-call(bf16[4,12800,512]{2,1,0:T(8,128)(2,1)} %get-tuple-element.826.p_ref, f32[4,5,10,512]{3,2,1,0:T(8,128)} %exponential_multiply_fusion.1.c_ref, s32[4,1,512]{2,1,0:T(1,128)} %copy.43.lab_ref, ...), custom_call_target="tpu_custom_call", output_to_operand_aliasing={{0}: (0, {})} | custom-call | flops 40265318400 | bytes 124518400 | tf_op jit(solution)/shard_map/head_bwd/pallas_call | solution.py:208
  1186.1 65.1 %head_bwd.5 = (bf16[4,12800,512]{2,1,0:T(8,128)(2,1)}, bf16[4,512,768]{2,1,0:T(8,128)(2,1)}) custom-call(bf16[4,12800,512]{2,1,0:T(8,128)(2,1)} %get-tuple-element.823.p_ref, f32[4,5,10,512]{3,2,1,0:T(8,128)} %exponential_multiply_fusion.2.c_ref, s32[4,1,512]{2,1,0:T(1,128)} %copy.41.lab_ref, ...), custom_call_target="tpu_custom_call", output_to_operand_aliasing={{0}: (0, {})} | custom-call | flops 40265318400 | bytes 124518400 | tf_op jit(solution)/shard_map/head_bwd/pallas_call | solution.py:208
  1255.1 65.6 %head_bwd.4 = (bf16[4,12800,512]{2,1,0:T(8,128)(2,1)}, bf16[4,512,768]{2,1,0:T(8,128)(2,1)}) custom-call(bf16[4,12800,512]{2,1,0:T(8,128)(2,1)} %get-tuple-element.819.p_ref, f32[4,5,10,512]{3,2,1,0:T(8,128)} %exponential_multiply_fusion.3.c_ref, s32[4,1,512]{2,1,0:T(1,128)} %copy.39.lab_ref, ...), custom_call_target="tpu_custom_call", output_to_operand_aliasing={{0}: (0, {})} | custom-call | flops 40265318400 | bytes 124518400 | tf_op jit(solution)/shard_map/head_bwd/pallas_call | solution.py:208
  1388.8 739.4 %while.55 = (s32[]{:T(128)}, bf16[512,768]{1,0:T(8,128)(2,1)S(1)}, bf16[512,768]{1,0:T(8,128)(2,1)S(1)}, bf16[512,768]{1,0:T(8,128)(2,1)S(1)}, bf16[17,512,768]{...) while((s32[]{:T(128)}, bf16[512,768]{1,0:T(8,128)(2,1)S(1)}, ...), condition=%wide.region_15.16_spmd, body=%wide.region_14.15_spmd.sunk | while | flops 7247757312 | bytes 26739136 | solution.py:453
  1411.6 103.7 %collective-permute-done.2 = bf16[512,768]{1,0:T(8,128)(2,1)} collective-permute-done((bf16[512,768]{1,0:T(8,128)(2,1)S(1)}, bf16[512,768]{1,0:T(8,128)(2,1)}, u32[]{:S(2)}, u32[]{:S(2)}) %collective-permute-start.2) | collective-permute-done | bytes 786464 | tf_op jit(solution)/shard_map/while/body/eval_jaxpr/ppermute | solution.py:443
  1659.2 20.0 layer_bwd.11
  1911.4 20.0 layer_bwd.11
  1997.2 19.9 layer_bwd.11
  2050.1 19.9 layer_bwd.11
  2076.6 20.0 layer_bwd.11
  2145.9 176.7 %table_grad.1 = f32[12576,768]{1,0:T(8,128)} custom-call(bf16[4,12800,512]{2,1,0:T(8,128)(2,1)} %get-tuple-element.835.refs_0_, bf16[4,12800,512]{2,1,0:T(8,128)(2,1)} %get-tuple-element.836.refs_1_, bf16[4,12800,512]{2,1,0:T(8,128)(2,1)} %get-tuple-element.837.refs_2_, bf16[4,12800,512]{2,1,0:T(8,128)(2,1)} %get-tuple-element.838.refs_3_, ...), custom_call_target="tpu_custom_call" | custom-call | flops 158242701312 | bytes 206045184 | tf_op jit(solution)/shard_map/table_grad/pallas_call | solution.py:242
  2329.2 52.0 %convolution_bitcast_fusion = f32[1,3072,768]{2,1,0:T(8,128)} fusion(bf16[17,512,3072]{2,1,0:T(8,128)(2,1)} %broadcast_dynamic-update-slice_fusion, bf16[17,512,768]{2,1,0:T(8,128)(2,1)} %broadcast_dynamic-update-slice_fusion.2), kind=kOutput, calls=%fused_computation.49 | convolution fusion | flops 41070624768 | bytes 76283904 | tf_op jit(solution)/shard_map/tf,td->fd/dot_general | solution.py:461
  2381.2 47.2 %convolution_bitcast_fusion.1 = f32[1,768,3072]{2,1,0:T(8,128)} fusion(bf16[17,512,768]{2,1,0:T(8,128)(2,1)S(1)} %bitcast.91, bf16[17,512,3072]{2,1,0:T(8,128)(2,1)} %broadcast_dynamic-update-slice_fusion.1), kind=kOutput, calls=%fused_computation.50 | convolution fusion | flops 41070624768 | bytes 76283904 | tf_op jit(solution)/shard_map/td,tf->df/dot_general | solution.py:460
  2439.2 80.5 %scatter_custom_fusion = f32[12576,768]{1,0:T(8,128)} fusion(f32[12576,768]{1,0:T(8,128)} %table_grad.1, s32[8192]{0:T(1024)} %bitcast.103, bf16[8192,768]{1,0:T(8,128)(2,1)} %bitcast.98), kind=kCustom, calls=%fused_computation.4 | custom fusion | flops 12582912 | bytes 51216384 | tf_op jit(solution)/shard_map/scatter-add | solution.py:465
  (591 shorter events, 1293.3 us)
Async XLA Ops:
  598.7 41.3 %collective-permute-start.8 = (bf16[4,512,768]{2,1,0:T(8,128)(2,1)}, bf16[4,512,768]{2,1,0:T(8,128)(2,1)}, u32[]{:S(2)}, u32[]{:S(2)}) collective-permute-start(bf16[4,512,768]{2,1,0:T(8,128)(2,1)} %collective-permute-done.7), channel_id=1, source_target_pairs={{1,0},{5,4}} | collective-permute-start | bytes 9437192 | tf_op jit(solution)/shard_map/ppermute | solution.py:367
  650.6 89.8 %collective-permute-start.16 = (bf16[4,512,768]{2,1,0:T(8,128)(2,1)}, bf16[4,512,768]{2,1,0:T(8,128)(2,1)S(1)}, u32[]{:S(2)}, u32[]{:S(2)}) collective-permute-start(bf16[4,512,768]{2,1,0:T(8,128)(2,1)} %get-tuple-element.910), channel_id=1, source_target_pairs={{3,1},{7,5}} | collective-permute-start | bytes 9437192 | tf_op jit(solution)/shard_map/ppermute | solution.py:367
  651.5 91.3 %collective-permute-start.15 = (bf16[4,512,768]{2,1,0:T(8,128)(2,1)}, bf16[4,512,768]{2,1,0:T(8,128)(2,1)}, u32[]{:S(2)}, u32[]{:S(2)}) collective-permute-start(bf16[4,512,768]{2,1,0:T(8,128)(2,1)} %get-tuple-element.910), channel_id=1, source_target_pairs={{3,2},{7,6}} | collective-permute-start | bytes 9437192 | tf_op jit(solution)/shard_map/ppermute | solution.py:367
  653.8 90.2 %collective-permute-start.13 = (bf16[4,512,768]{2,1,0:T(8,128)(2,1)}, bf16[4,512,768]{2,1,0:T(8,128)(2,1)}, u32[]{:S(2)}, u32[]{:S(2)}) collective-permute-start(bf16[4,512,768]{2,1,0:T(8,128)(2,1)} %get-tuple-element.911), channel_id=1, source_target_pairs={{3,1},{7,5}} | collective-permute-start | bytes 9437192 | tf_op jit(solution)/shard_map/ppermute | solution.py:367
  656.1 89.2 %collective-permute-start.10 = (bf16[4,512,768]{2,1,0:T(8,128)(2,1)}, bf16[4,512,768]{2,1,0:T(8,128)(2,1)}, u32[]{:S(2)}, u32[]{:S(2)}) collective-permute-start(bf16[4,512,768]{2,1,0:T(8,128)(2,1)} %get-tuple-element.912), channel_id=1, source_target_pairs={{3,1},{7,5}} | collective-permute-start | bytes 9437192 | tf_op jit(solution)/shard_map/ppermute | solution.py:367
  739.6 73.6 %collective-permute-start.12 = (bf16[4,512,768]{2,1,0:T(8,128)(2,1)}, bf16[4,512,768]{2,1,0:T(8,128)(2,1)S(1)}, u32[]{:S(2)}, u32[]{:S(2)}) collective-permute-start(bf16[4,512,768]{2,1,0:T(8,128)(2,1)} %get-tuple-element.911), channel_id=1, source_target_pairs={{3,2},{7,6}} | collective-permute-start | bytes 9437192 | tf_op jit(solution)/shard_map/ppermute | solution.py:367
  740.5 72.8 %collective-permute-start.9 = (bf16[4,512,768]{2,1,0:T(8,128)(2,1)}, bf16[4,512,768]{2,1,0:T(8,128)(2,1)}, u32[]{:S(2)}, u32[]{:S(2)}) collective-permute-start(bf16[4,512,768]{2,1,0:T(8,128)(2,1)} %get-tuple-element.912), channel_id=1, source_target_pairs={{3,2},{7,6}} | collective-permute-start | bytes 9437192 | tf_op jit(solution)/shard_map/ppermute | solution.py:367
  742.8 70.5 %collective-permute-start.17 = (bf16[4,512,768]{2,1,0:T(8,128)(2,1)S(1)}, bf16[4,512,768]{2,1,0:T(8,128)(2,1)}, u32[]{:S(2)}, u32[]{:S(2)}) collective-permute-start(bf16[4,512,768]{2,1,0:T(8,128)(2,1)S(1)} %collective-permute-done.16), channel_id=1, source_target_pairs={{1,0},{5,4}} | collective-permute-start | bytes 9437192 | tf_op jit(solution)/shard_map/ppermute | solution.py:367
  744.1 69.2 %collective-permute-start.14 = (bf16[4,512,768]{2,1,0:T(8,128)(2,1)}, bf16[4,512,768]{2,1,0:T(8,128)(2,1)}, u32[]{:S(2)}, u32[]{:S(2)}) collective-permute-start(bf16[4,512,768]{2,1,0:T(8,128)(2,1)} %collective-permute-done.13), channel_id=1, source_target_pairs={{1,0},{5,4}} | collective-permute-start | bytes 9437192 | tf_op jit(solution)/shard_map/ppermute | solution.py:367
  745.4 67.9 %collective-permute-start.11 = (bf16[4,512,768]{2,1,0:T(8,128)(2,1)}, bf16[4,512,768]{2,1,0:T(8,128)(2,1)}, u32[]{:S(2)}, u32[]{:S(2)}) collective-permute-start(bf16[4,512,768]{2,1,0:T(8,128)(2,1)} %collective-permute-done.10), channel_id=1, source_target_pairs={{1,0},{5,4}} | collective-permute-start | bytes 9437192 | tf_op jit(solution)/shard_map/ppermute | solution.py:367
  1114.6 207.9 %collective-permute-start.24 = (bf16[4,512,768]{2,1,0:T(8,128)(2,1)}, bf16[4,512,768]{2,1,0:T(8,128)(2,1)S(1)}, u32[]{:S(2)}, u32[]{:S(2)}) collective-permute-start(bf16[4,512,768]{2,1,0:T(8,128)(2,1)} %get-tuple-element.831), channel_id=1, source_target_pairs={{0,1},{2,3},{4,5},{6,7}} | collective-permute-start | bytes 9437192 | tf_op jit(solution)/shard_map/ppermute | solution.py:367
  1182.2 145.5 %collective-permute-start.22 = (bf16[4,512,768]{2,1,0:T(8,128)(2,1)}, bf16[4,512,768]{2,1,0:T(8,128)(2,1)}, u32[]{:S(2)}, u32[]{:S(2)}) collective-permute-start(bf16[4,512,768]{2,1,0:T(8,128)(2,1)} %get-tuple-element.828), channel_id=1, source_target_pairs={{0,1},{2,3},{4,5},{6,7}} | collective-permute-start | bytes 9437192 | tf_op jit(solution)/shard_map/ppermute | solution.py:367
  1251.2 83.3 %collective-permute-start.20 = (bf16[4,512,768]{2,1,0:T(8,128)(2,1)}, bf16[4,512,768]{2,1,0:T(8,128)(2,1)}, u32[]{:S(2)}, u32[]{:S(2)}) collective-permute-start(bf16[4,512,768]{2,1,0:T(8,128)(2,1)} %get-tuple-element.825), channel_id=1, source_target_pairs={{0,1},{2,3},{4,5},{6,7}} | collective-permute-start | bytes 9437192 | tf_op jit(solution)/shard_map/ppermute | solution.py:367
  1393.4 121.8 %collective-permute-start.2 = (bf16[512,768]{1,0:T(8,128)(2,1)S(1)}, bf16[512,768]{1,0:T(8,128)(2,1)}, u32[]{:S(2)}, u32[]{:S(2)}) collective-permute-start(bf16[512,768]{1,0:T(8,128)(2,1)S(1)} %copy.103), channel_id=1, source_target_pairs={{1,0},{2,1},{3,2},{5,4},{6,5},{7,6}} | collective-permute-start | bytes 2359304 | tf_op jit(solution)/shard_map/while/body/eval_jaxpr/ppermute | solution.py:443
  1638.6 40.6 %collective-permute-start.3 = (bf16[512,768]{1,0:T(8,128)(2,1)S(1)}, bf16[512,768]{1,0:T(8,128)(2,1)}, u32[]{:S(2)}, u32[]{:S(2)}) collective-permute-start(bf16[512,768]{1,0:T(8,128)(2,1)S(1)} %copy.103), channel_id=1, source_target_pairs={{0,2},{4,6}} | collective-permute-start | bytes 2359304 | tf_op jit(solution)/shard_map/while/body/eval_jaxpr/ppermute | solution.py:367
  1708.2 27.2 %collective-permute-start.3 = (bf16[512,768]{1,0:T(8,128)(2,1)S(1)}, bf16[512,768]{1,0:T(8,128)(2,1)}, u32[]{:S(2)}, u32[]{:S(2)}) collective-permute-start(bf16[512,768]{1,0:T(8,128)(2,1)S(1)} %copy.103), channel_id=1, source_target_pairs={{0,2},{4,6}} | collective-permute-start | bytes 2359304 | tf_op jit(solution)/shard_map/while/body/eval_jaxpr/ppermute | solution.py:367
  1764.5 27.1 %collective-permute-start.3 = (bf16[512,768]{1,0:T(8,128)(2,1)S(1)}, bf16[512,768]{1,0:T(8,128)(2,1)}, u32[]{:S(2)}, u32[]{:S(2)}) collective-permute-start(bf16[512,768]{1,0:T(8,128)(2,1)S(1)} %copy.103), channel_id=1, source_target_pairs={{0,2},{4,6}} | collective-permute-start | bytes 2359304 | tf_op jit(solution)/shard_map/while/body/eval_jaxpr/ppermute | solution.py:367
  1820.8 27.1 %collective-permute-start.3 = (bf16[512,768]{1,0:T(8,128)(2,1)S(1)}, bf16[512,768]{1,0:T(8,128)(2,1)}, u32[]{:S(2)}, u32[]{:S(2)}) collective-permute-start(bf16[512,768]{1,0:T(8,128)(2,1)S(1)} %copy.103), channel_id=1, source_target_pairs={{0,2},{4,6}} | collective-permute-start | bytes 2359304 | tf_op jit(solution)/shard_map/while/body/eval_jaxpr/ppermute | solution.py:367
  1877.3 27.0 %collective-permute-start.3 = (bf16[512,768]{1,0:T(8,128)(2,1)S(1)}, bf16[512,768]{1,0:T(8,128)(2,1)}, u32[]{:S(2)}, u32[]{:S(2)}) collective-permute-start(bf16[512,768]{1,0:T(8,128)(2,1)S(1)} %copy.103), channel_id=1, source_target_pairs={{0,2},{4,6}} | collective-permute-start | bytes 2359304 | tf_op jit(solution)/shard_map/while/body/eval_jaxpr/ppermute | solution.py:367
  1906.6 24.9 collective-permute-start.3
  1933.8 26.8 %collective-permute-start.3 = (bf16[512,768]{1,0:T(8,128)(2,1)S(1)}, bf16[512,768]{1,0:T(8,128)(2,1)}, u32[]{:S(2)}, u32[]{:S(2)}) collective-permute-start(bf16[512,768]{1,0:T(8,128)(2,1)S(1)} %copy.103), channel_id=1, source_target_pairs={{0,2},{4,6}} | collective-permute-start | bytes 2359304 | tf_op jit(solution)/shard_map/while/body/eval_jaxpr/ppermute | solution.py:367
  1962.9 24.6 collective-permute-start.3
  1989.9 27.3 %collective-permute-start.3 = (bf16[512,768]{1,0:T(8,128)(2,1)S(1)}, bf16[512,768]{1,0:T(8,128)(2,1)}, u32[]{:S(2)}, u32[]{:S(2)}) collective-permute-start(bf16[512,768]{1,0:T(8,128)(2,1)S(1)} %copy.103), channel_id=1, source_target_pairs={{0,2},{4,6}} | collective-permute-start | bytes 2359304 | tf_op jit(solution)/shard_map/while/body/eval_jaxpr/ppermute | solution.py:367
  2138.9 289.5 %collective-permute-start.26 = (bf16[16,512,768]{2,1,0:T(8,128)(2,1)}, bf16[16,512,768]{2,1,0:T(8,128)(2,1)}, u32[]{:S(2)}, u32[]{:S(2)}) collective-permute-start(bf16[16,512,768]{2,1,0:T(8,128)(2,1)} %slice.149), channel_id=1, source_target_pairs={{0,1},{2,3},{4,5},{6,7}} | collective-permute-start | bytes 37748744 | tf_op jit(solution)/shard_map/ppermute | solution.py:367
  (118 other events, 2615.8 us)

commit v2 on v1

v2 whole, which is shorter than its diff:
```python
import functools
import jax
import jax.numpy as jnp
from jax import lax
from jax.experimental import pallas as pl
from jax.experimental.pallas import tpu as pltpu
from jax.sharding import PartitionSpec as P

NORM_EPS = 1e-6
LOG2E = 1.4426950408889634
LN2 = 0.6931471805599453
GELU_K = 0.7978845608028654
GELU_A = 0.044715
SUB = 512
SUBS = 5
STAGES = 4
MESH = pl.DeviceIdType.MESH
PIPE_CAP = 60 * 1024 * 1024
TILE = SUB * SUBS
GROUPS = 4
PARTS = 6
V_TILE = 640
VMEM_CAP = 56 * 1024 * 1024
BF = jnp.bfloat16
F32 = jnp.float32


def norm_f32(act_rows):
    acts_f = act_rows.astype(F32)
    return acts_f * lax.rsqrt(jnp.mean(acts_f * acts_f, axis=-1, keepdims=True) + NORM_EPS)


def gelu_hidden(pre):
    inner = jnp.tanh(pre * (GELU_K + (GELU_K * GELU_A) * (pre * pre)))
    half = 0.5 * pre
    return (half + half * inner).astype(BF)


def remote(src, dst, send_sem, recv_sem, target):
    return pltpu.make_async_remote_copy(src_ref=src, dst_ref=dst, send_sem=send_sem, recv_sem=recv_sem,
                                        device_id=(lax.axis_index("dp"), target), device_id_type=MESH)


def forward_pipe_body(here_ref, w1_ref, w2_ref, save_ref, last_ref, n_ref, recv, local, out_buf, w1, w2,
                      w_sem, local_sem, recv_sem, send_sem, far_sem, save_sem, last_sem, n_sem):
    stage = lax.axis_index("stage")
    count = recv.shape[0]
    end = STAGES - 1
    ffn = w1.shape[1]
    width = ffn // PARTS
    loads = [pltpu.make_async_copy(w1_ref, w1, w_sem.at[0]), pltpu.make_async_copy(w2_ref, w2, w_sem.at[1])]
    for load in loads:
        load.start()

    def far(m):
        return remote(here_ref.at[m], recv.at[m], far_sem.at[m], recv_sem.at[m], 0)

    def onward(m):
        return remote(out_buf.at[m], recv.at[m], send_sem.at[m], recv_sem.at[m], lax.rem(stage + 1, STAGES))

    def begin(m, _):
        @pl.when(stage == 2)
        def _():
            far(m).start()

        @pl.when(stage == 0)
        def _():
            pltpu.make_async_copy(here_ref.at[m], local.at[m], local_sem.at[m]).start()
        return 0

    lax.fori_loop(0, count, begin, 0)
    for load in loads:
        load.wait()

    def chunk(m, _):
        onward(m).wait_recv()

        @pl.when(stage == 0)
        def _():
            pltpu.make_async_copy(here_ref.at[m], local.at[m], local_sem.at[m]).wait()
            recv[m] = recv[m] + local[m]

        pltpu.make_async_copy(recv.at[m], save_ref.at[m], save_sem.at[m]).start()
        x = recv[m]
        total = None
        for part in range(PARTS):
            cols = slice(part * width, (part + 1) * width)
            hidden = gelu_hidden(jnp.dot(x, w1[:, cols], preferred_element_type=F32))
            term = jnp.dot(hidden, w2[cols, :], preferred_element_type=F32)
            total = term if total is None else total + term
        out_buf[m] = (x.astype(F32) + total).astype(BF)

        @pl.when(stage < end)
        def _():
            onward(m).start()

        @pl.when(stage == end)
        def _():
            local[m] = norm_f32(out_buf[m]).astype(BF)
            pltpu.make_async_copy(out_buf.at[m], last_ref.at[m], last_sem.at[m]).start()
            pltpu.make_async_copy(local.at[m], n_ref.at[m], n_sem.at[m]).start()
        return 0

    lax.fori_loop(0, count, chunk, 0)

    def finish(m, _):
        pltpu.make_async_copy(recv.at[m], save_ref.at[m], save_sem.at[m]).wait()

        @pl.when(stage == 2)
        def _():
            far(m).wait_send()

        @pl.when(stage < end)
        def _():
            onward(m).wait_send()

        @pl.when(stage == end)
        def _():
            pltpu.make_async_copy(out_buf.at[m], last_ref.at[m], last_sem.at[m]).wait()
            pltpu.make_async_copy(local.at[m], n_ref.at[m], n_sem.at[m]).wait()
        return 0

    lax.fori_loop(0, count, finish, 0)


def forward_pipe(chip_rows, w1, w2):
    count, rows, dim = chip_rows.shape
    any_spec = pl.BlockSpec(memory_space=pl.ANY)
    store = jax.ShapeDtypeStruct(chip_rows.shape, BF)
    dma = pltpu.SemaphoreType.DMA
    return pl.pallas_call(
        forward_pipe_body,
        in_specs=[any_spec] * 3,
        out_specs=[any_spec] * 3,
        out_shape=[store] * 3,
        scratch_shapes=[pltpu.VMEM(chip_rows.shape, BF)] * 3 + [pltpu.VMEM(w1.shape, BF), pltpu.VMEM(w2.shape, BF), dma((2,))] + [dma((count,))] * 7,
        compiler_params=pltpu.CompilerParams(vmem_limit_bytes=PIPE_CAP, has_side_effects=True),
        cost_estimate=pl.CostEstimate(flops=4 * count * rows * dim * w1.shape[1], bytes_accessed=4 * dim * w1.shape[1], transcendentals=0),
        name="forward_pipe",
    )(chip_rows, w1, w2)


def backward_pipe_body(x_ref, top_ref, w1_ref, w1t_ref, w2t_ref, g_ref, h_ref, gp_ref, dx_ref, recv, x_buf, h_buf, gp_buf, gin_buf, w1, w1t, w2t,
                       w_sem, top_sem, x_sem, recv_sem, send_sem, g_sem, h_sem, gp_sem, dx_sem, dx_recv):
    stage = lax.axis_index("stage")
    count = recv.shape[0]
    end = STAGES - 1
    width = w1.shape[1] // PARTS
    loads = [pltpu.make_async_copy(src, dst, w_sem.at[i]) for i, (src, dst) in enumerate(((w1_ref, w1), (w1t_ref, w1t), (w2t_ref, w2t)))]
    for load in loads:
        load.start()

    def load_top(m):
        return pltpu.make_async_copy(top_ref.at[m], recv.at[m], top_sem.at[m])

    def load_x(m):
        return pltpu.make_async_copy(x_ref.at[m], x_buf.at[lax.rem(m, 2)], x_sem.at[m])

    def save_g(m):
        return pltpu.make_async_copy(recv.at[m], g_ref.at[m], g_sem.at[m])

    def save_h(m):
        return pltpu.make_async_copy(h_buf.at[lax.rem(m, 2)], h_ref.at[m], h_sem.at[m])

    def save_gp(m):
        return pltpu.make_async_copy(gp_buf.at[lax.rem(m, 2)], gp_ref.at[m], gp_sem.at[m])

    def save_dx(m):
        return pltpu.make_async_copy(gin_buf.at[lax.rem(m, 2)], dx_ref.at[m], dx_sem.at[m])

    def onward(m):
        return remote(gin_buf.at[lax.rem(m, 2)], recv.at[m], send_sem.at[m], recv_sem.at[m], lax.rem(stage + end, STAGES))

    def cross(m):
        return remote(gin_buf.at[lax.rem(m, 2)], dx_ref.at[m], send_sem.at[m], dx_recv.at[m], 2)

    def begin(m, _):
        @pl.when(stage == end)
        def _():
            load_top(m).start()
        return 0

    lax.fori_loop(0, count, begin, 0)
    load_x(0).start()
    for load in loads:
        load.wait()

    def drain(m):
        save_h(m).wait()
        save_gp(m).wait()

        @pl.when(stage > 0)
        def _():
            onward(m).wait_send()

        @pl.when(stage == 0)
        def _():
            cross(m).wait_send()
            save_dx(m).wait()

    def chunk(m, _):
        slot = lax.rem(m, 2)

        @pl.when(m + 1 < count)
        def _():
            load_x(m + 1).start()

        @pl.when(stage == end)
        def _():
            load_top(m).wait()

        @pl.when(stage < end)
        def _():
            onward(m).wait_recv()

        save_g(m).start()
        load_x(m).wait()

        @pl.when(m >= 2)
        def _():
            drain(m - 2)

        x = x_buf[slot]
        grad_out = recv[m]
        total = None
        for part in range(PARTS):
            cols = slice(part * width, (part + 1) * width)
            pre = jnp.dot(x, w1[:, cols], preferred_element_type=F32)
            grad_hidden = jnp.dot(grad_out, w2t[:, cols], preferred_element_type=F32)
            sq = pre * pre
            inner = jnp.tanh(pre * (GELU_K + (GELU_K * GELU_A) * sq))
            side = 0.5 + 0.5 * inner
            bend = (0.5 - 0.5 * inner * inner) * (GELU_K + (3.0 * GELU_K * GELU_A) * sq)
            h_buf[slot, :, cols] = (pre * side).astype(BF)
            grad_pre = (grad_hidden * (side + pre * bend)).astype(BF)
            gp_buf[slot, :, cols] = grad_pre
            term = jnp.dot(grad_pre, w1t[cols, :], preferred_element_type=F32)
            total = term if total is None else total + term
        gin_buf[slot] = (grad_out.astype(F32) + total).astype(BF)
        save_h(m).start()
        save_gp(m).start()

        @pl.when(stage > 0)
        def _():
            onward(m).start()

        @pl.when(stage == 0)
        def _():
            cross(m).start()
            save_dx(m).start()
        return 0

    lax.fori_loop(0, count, chunk, 0)
    drain(count - 2)
    drain(count - 1)

    def finish(m, _):
        save_g(m).wait()

        @pl.when(stage == 2)
        def _():
            cross(m).wait_recv()
        return 0

    lax.fori_loop(0, count, finish, 0)


def backward_pipe(saved_in, grad_last, w1, w1t, w2t):
    count, rows, dim = saved_in.shape
    ffn = w1.shape[1]
    any_spec = pl.BlockSpec(memory_space=pl.ANY)
    store = jax.ShapeDtypeStruct(saved_in.shape, BF)
    wide = jax.ShapeDtypeStruct((count, rows, ffn), BF)
    dma = pltpu.SemaphoreType.DMA
    return pl.pallas_call(
        backward_pipe_body,
        in_specs=[any_spec] * 5,
        out_specs=[any_spec] * 4,
        out_shape=[store, wide, wide, store],
        scratch_shapes=[
            pltpu.VMEM(saved_in.shape, BF),
            pltpu.VMEM((2, rows, dim), BF),
            pltpu.VMEM((2, rows, ffn), BF),
            pltpu.VMEM((2, rows, ffn), BF),
            pltpu.VMEM((2, rows, dim), BF),
            pltpu.VMEM(w1.shape, BF), pltpu.VMEM(w1t.shape, BF), pltpu.VMEM(w2t.shape, BF),
            dma((3,)),
        ] + [dma((count,))] * 9,
        compiler_params=pltpu.CompilerParams(vmem_limit_bytes=PIPE_CAP, has_side_effects=True),
        cost_estimate=pl.CostEstimate(flops=6 * count * rows * dim * ffn, bytes_accessed=4 * dim * ffn, transcendentals=0),
        name="backward_pipe",
    )(saved_in, grad_last, w1, w1t, w2t)


def head_forward_body(n_valid, log_scale, n_ref, e_ref, lab_ref, p_ref, m_ref, st_ref, run):
    tile, chunk = pl.program_id(0), pl.program_id(1)

    @pl.when(tile == 0)
    def _():
        run[chunk, 0:1, :] = jnp.full((1, run.shape[2]), -jnp.inf, F32)
        run[chunk, 1:3, :] = jnp.zeros((2, run.shape[2]), F32)

    n_rows = n_ref[0]
    lab = lab_ref[0] - tile * TILE
    top, tot, hit = run[chunk, 0:1, :], run[chunk, 1:2, :], run[chunk, 2:3, :]
    rows = lax.broadcasted_iota(jnp.int32, (SUB, n_rows.shape[1]), 0)
    for sub in range(SUBS):
        cut = slice(sub * SUB, (sub + 1) * SUB)
        logit = jnp.dot(e_ref[cut, :], n_rows, preferred_element_type=F32) * log_scale
        if sub == SUBS - 1:
            logit = jnp.where(rows < n_valid - tile * TILE - sub * SUB, logit, -jnp.inf)
        hit = hit + jnp.sum(jnp.where(rows == lab - sub * SUB, logit, 0.0), axis=0, keepdims=True)
        new_top = jnp.maximum(top, jnp.max(logit, axis=0, keepdims=True))
        expo = jnp.exp2(logit - new_top)
        tot = tot * jnp.exp2(top - new_top) + jnp.sum(expo, axis=0, keepdims=True)
        p_ref[0, cut, :] = expo.astype(BF)
        m_ref[0, 0, sub:sub + 1, :] = new_top
        top = new_top
    run[chunk, 0:1, :] = top
    run[chunk, 1:2, :] = tot
    run[chunk, 2:3, :] = hit
    st_ref[0, 0:1, :] = top
    st_ref[0, 1:2, :] = tot
    st_ref[0, 2:3, :] = hit


def head_forward(normed, emb_pad, labels, n_valid, log_scale):
    chunks, dim, rows = normed.shape
    padded = emb_pad.shape[0]
    tiles = padded // TILE
    row = pl.BlockSpec((1, 1, rows), lambda t, c: (c, 0, 0))
    return pl.pallas_call(
        functools.partial(head_forward_body, n_valid, log_scale),
        grid=(tiles, chunks),
        in_specs=[
            pl.BlockSpec((1, dim, rows), lambda t, c: (c, 0, 0)),
            pl.BlockSpec((TILE, dim), lambda t, c: (t, 0)),
            row,
        ],
        out_specs=[
            pl.BlockSpec((1, TILE, rows), lambda t, c: (c, t, 0)),
            pl.BlockSpec((1, 1, SUBS, rows), lambda t, c: (c, t, 0, 0)),
            pl.BlockSpec((1, 3, rows), lambda t, c: (c, 0, 0)),
        ],
        out_shape=[
            jax.ShapeDtypeStruct((chunks, padded, rows), BF),
            jax.ShapeDtypeStruct((chunks, tiles, SUBS, rows), F32),
            jax.ShapeDtypeStruct((chunks, 3, rows), F32),
        ],
        scratch_shapes=[pltpu.VMEM((chunks, 3, rows), F32)],
        compiler_params=pltpu.CompilerParams(vmem_limit_bytes=VMEM_CAP),
        cost_estimate=pl.CostEstimate(flops=2 * chunks * rows * dim * padded, bytes_accessed=padded * (2 * dim + 2 * rows * chunks), transcendentals=rows * chunks * padded),
        name="head_fwd",
    )(normed, emb_pad, labels)


def head_backward_body(p_ref, c_ref, lab_ref, g_ref, et_ref, d_ref, out_ref, acc_ref):
    tile, chunk = pl.program_id(0), pl.program_id(1)
    lab = lab_ref[0] - tile * TILE
    gain = g_ref[0]
    rows = lax.broadcasted_iota(jnp.int32, (SUB, lab.shape[1]), 0)
    total = None
    for sub in range(SUBS):
        cut = slice(sub * SUB, (sub + 1) * SUB)
        prob = p_ref[0, cut, :].astype(F32) * c_ref[0, 0, sub:sub + 1, :]
        delta = jnp.where(rows == lab - sub * SUB, gain, prob).astype(BF)
        d_ref[0, cut, :] = delta
        term = jnp.dot(et_ref[:, cut], delta, preferred_element_type=F32)
        total = term if total is None else total + term

    @pl.when(tile == 0)
    def _():
        acc_ref[chunk] = total

    @pl.when(tile > 0)
    def _():
        acc_ref[chunk] += total

    @pl.when(tile == pl.num_programs(0) - 1)
    def _():
        out_ref[0] = acc_ref[chunk].T.astype(BF)


def head_backward(expo, coef, labels, gain, emb_t):
    chunks, padded, rows = expo.shape
    dim = emb_t.shape[0]
    tiles = padded // TILE
    row = pl.BlockSpec((1, 1, rows), lambda t, c: (c, 0, 0))
    block = pl.BlockSpec((1, TILE, rows), lambda t, c: (c, t, 0))
    end = tiles - 1
    return pl.pallas_call(
        head_backward_body,
        grid=(tiles, chunks),
        in_specs=[
            block,
            pl.BlockSpec((1, 1, SUBS, rows), lambda t, c: (c, t, 0, 0)),
            row,
            row,
            pl.BlockSpec((dim, TILE), lambda t, c: (0, t)),
        ],
        out_specs=[block, pl.BlockSpec((1, rows, dim), lambda t, c: (c * (t // end), 0, 0))],
        out_shape=[jax.ShapeDtypeStruct(expo.shape, BF), jax.ShapeDtypeStruct((chunks, rows, dim), BF)],
        scratch_shapes=[pltpu.VMEM((chunks, dim, rows), F32)],
        input_output_aliases={0: 0},
        compiler_params=pltpu.CompilerParams(vmem_limit_bytes=VMEM_CAP),
        cost_estimate=pl.CostEstimate(flops=2 * chunks * rows * dim * padded, bytes_accessed=padded * (2 * dim + 4 * rows * chunks), transcendentals=0),
        name="head_bwd",
    )(expo, coef, labels, gain, emb_t)


def table_grad_body(groups, *refs):
    deltas, normed, out_ref = refs[:groups], refs[groups:2 * groups], refs[2 * groups]
    total = None
    for d_ref, n_ref in zip(deltas, normed):
        for chunk in range(d_ref.shape[0]):
            term = jnp.dot(d_ref[chunk], n_ref[chunk], preferred_element_type=F32)
            total = term if total is None else total + term
    out_ref[...] = total


def table_grad(deltas, normed, slice_rows, v_tile):
    chunks, rows, dim = normed[0].shape
    groups = len(deltas)
    tokens = groups * chunks * rows
    return pl.pallas_call(
        functools.partial(table_grad_body, groups),
        grid=(-(-slice_rows // v_tile),),
        in_specs=[pl.BlockSpec((chunks, v_tile, rows), lambda v: (0, v, 0))] * groups
        + [pl.BlockSpec((chunks, rows, dim), lambda v: (0, 0, 0), pipeline_mode=pl.Buffered(1))] * groups,
        out_specs=pl.BlockSpec((v_tile, dim), lambda v: (v, 0)),
        out_shape=jax.ShapeDtypeStruct((slice_rows, dim), F32),
        compiler_params=pltpu.CompilerParams(vmem_limit_bytes=VMEM_CAP),
        cost_estimate=pl.CostEstimate(flops=2 * slice_rows * dim * tokens, bytes_accessed=2 * slice_rows * tokens, transcendentals=0),
        name="table_grad",
    )(*deltas, *normed)


def solution(mesh):

    def stage_body(token_ids, label_ids, emb_rows, w_in, w_out):
        stage = lax.axis_index("stage")
        micro_count, micro_tokens = token_ids.shape
        slice_rows, dim = emb_rows.shape
        scale = dim ** -0.5
        w1, w2 = w_in[0], w_out[0]
        row_start = stage * slice_rows
        padded = -(-slice_rows // TILE) * TILE
        per = micro_count // GROUPS

        def hop(value, *pairs):
            return lax.ppermute(value, "stage", pairs)

        local_tok = token_ids - row_start
        tok_here = (local_tok >= 0) & (local_tok < slice_rows)
        looked_up = jnp.take(emb_rows, jnp.clip(local_tok, 0, slice_rows - 1), axis=0)
        own_rows = jnp.where(tok_here[..., None], looked_up, 0)
        chip_rows = own_rows + hop(own_rows, (1, 0), (3, 2))

        emb_pad = jnp.pad(emb_rows, ((0, padded - slice_rows), (0, 0)))
        emb_t = emb_pad.T
        local_lab = label_ids - row_start
        labels = jnp.where((local_lab >= 0) & (local_lab < slice_rows), local_lab, -1)[:, None]

        saved_in, last_out, normed = forward_pipe(chip_rows, w1, w2)

        cuts = [slice(g * per, (g + 1) * per) for g in range(GROUPS)]
        n_parts, expo, maxes, stats = [], [], [], []
        for cut in cuts:
            own = normed[cut]
            near = hop(own, (3, 2))
            cross = hop(own, (3, 1))
            final = hop(cross, (1, 0))
            part = jnp.where(stage == 3, own, jnp.where(stage == 2, near, jnp.where(stage == 1, cross, final)))
            n_parts.append(part)
            res = head_forward(part.transpose(0, 2, 1), emb_pad, labels[cut], slice_rows, scale * LOG2E)
            expo.append(res[0])
            maxes.append(res[1])
            stats.append(res[2])

        every = lax.all_gather(jnp.concatenate(stats), "stage")
        top = jnp.max(every[:, :, 0], axis=0)
        denom = jnp.sum(every[:, :, 1] * jnp.exp2(every[:, :, 0] - top), axis=0)
        hit = jnp.sum(every[:, :, 2], axis=0)
        mean_loss = (jnp.sum(jnp.log2(denom) + top - hit) * (LN2 / (micro_count * micro_tokens))).reshape(1)
        ratio = scale / denom
        gain = ((jnp.exp2(hit - top) / denom - 1.0) * scale)[:, None]

        deltas, grad_last = [], []
        for g, cut in enumerate(cuts):
            coef = jnp.exp2(maxes[g] - top[cut, None, None]) * ratio[cut, None, None]
            delta, part = head_backward(expo[g], coef, labels[cut], gain[cut], emb_t)
            deltas.append(delta)
            near = hop(part, (0, 1), (2, 3)).astype(F32)
            pair = part.astype(F32) + near
            far = hop(pair.astype(BF), (1, 3)).astype(F32)
            _, pull = jax.vjp(norm_f32, last_out[cut])
            grad_last.append(pull(pair + far)[0])
        grad_last = jnp.concatenate(grad_last)

        grad_head = table_grad(deltas, n_parts, slice_rows, V_TILE)

        grads, hidden, grad_pre, dx_rows = backward_pipe(saved_in, grad_last, w1, w1.T, w2.T)

        def flat(value):
            return value.reshape(-1, value.shape[2])

        grad_first = jnp.einsum("td,tf->df", flat(saved_in), flat(grad_pre), preferred_element_type=F32)
        grad_second = jnp.einsum("tf,td->fd", flat(hidden), flat(grads), preferred_element_type=F32)
        dx_rows = jnp.where(stage % 2 == 0, dx_rows, hop(dx_rows, (0, 1), (2, 3)))
        seg = jnp.where(tok_here, local_tok, slice_rows).reshape(-1)
        grad_emb = grad_head.at[seg].add(dx_rows.reshape(-1, dim).astype(F32), mode="drop")
        return mean_loss, grad_first[None], grad_second[None], grad_emb

    return jax.shard_map(
        stage_body,
        mesh=mesh,
        in_specs=(P("dp", None), P("dp", None), P("stage", None), P("stage", None, None), P("stage", None, None)),
        out_specs=(P("dp"), P(("dp", "stage"), None, None), P(("dp", "stage"), None, None), P(("dp", "stage"), None)),
        check_vma=False,
    )
```

time: 2540 us -> 1800 us (0.71)
  starting transfers between devices: 363 us -> 47.3 us
  local copies, waits for them, and re-layouts: 321 us -> 164 us
  waiting for transfers between devices: 225 us -> 88.1 us
  Pallas kernels: 1290 us -> 1180 us
    ppermute x69 -> x22, starting transfers between devices: 230 us -> 47.3 us  [hop(): return lax.ppermute(value, 'stage', pairs)]
    ppermute x46 -> x0, starting transfers between devices: 133 us -> none  [the longest x22 102 us: fwd_tick(): next_moved = lax.ppermute(out, 'stage', fwd_pairs)]
    pallas_call x47 -> x2, Pallas kernels: 584 us -> 460 us  [the longest x1 309 us: backward_pipe(): pl.pallas_call(backward_pipe_body, in_specs=[any_spec] * 5, out_specs=[an...]
    while x92 -> x0, local copies, waits for them, and re-layouts: 105 us -> none
    ppermute x46 -> x0, waiting for transfers between devices: 104 us -> none  [the longest x24 104 us: bwd_tick(): next_moved = lax.ppermute(grad_in, 'stage', bwd_pairs)]
    another operation x70 -> x0, local copies, waits for them, and re-layouts: 37.1 us -> none
    ppermute x69 -> x22, waiting for transfers between devices: 121 us -> 88.1 us  [hop(): return lax.ppermute(value, 'stage', pairs)]
    squeeze x23 -> x0, local copies, waits for them, and re-layouts: 26.1 us -> none  [take(): return lax.dynamic_index_in_dim(store, slot, 0, keepdims=False)]
  transfers between devices with their start and end apart: 115 -> 22, of which waited for: 18 -> 2; matrix products, arithmetic and copies ran while one was open for 12% -> 12% of each run, Pallas kernels for 41% -> 25%
where the time goes in v2:
time: 1800 us; the launch traced here: 1780 us
  Pallas kernels  1180 us (66%)
  other arithmetic  183 us (10%)
  local copies, waits for them, and re-layouts  164 us (9%)
  matrix products  97.3 us (5%)
  waiting for transfers between devices  88.1 us (5%)
  starting transfers between devices  47.3 us (3%)
    pallas_call x1, Pallas kernels, backward_pipe(): pl.pallas_call(backward_pipe_body, in_specs=[any_spec] * 5, out_specs=[an...  309 us
    pallas_call x4, Pallas kernels, head_forward(): pl.pallas_call(functools.partial(head_forward_body, n_valid, log_scale),...  283 us
    pallas_call x4, Pallas kernels, head_backward(): pl.pallas_call(head_backward_body, grid=(tiles, chunks), in_specs=[block,...  261 us
    pallas_call x1, Pallas kernels, table_grad(): pl.pallas_call(functools.partial(table_grad_body, groups), grid=(-(-slice...  177 us
    pallas_call x1, Pallas kernels, forward_pipe(): pl.pallas_call(forward_pipe_body, in_specs=[any_spec] * 3, out_specs=[any...  151 us
    ppermute x22, waiting for transfers between devices, hop(): return lax.ppermute(value, 'stage', pairs)  88.1 us
    scatter-add x1, other arithmetic, stage_body(): grad_head.at[seg].add(dx_rows.reshape(-1, dim).astype(F32), mode='drop')  80.2 us
    unnamed x64, local copies, waits for them, and re-layouts  68.7 us
  transfers between devices with their start and end apart: 22, of which 2 were waited for; matrix products, arithmetic and copies ran while one was open for 12% of the time, Pallas kernels for 25%

profile of v2, /device:TPU:0, one launch (start us, length us, event | category | flops | bytes accessed | tf_op | source)
XLA Modules:
  0.0 1779.5 jit_solution(12581259449703588706)
XLA Ops:
  2.8 46.0 %gather_fusion = bf16[8192,768]{1,0:T(8,128)(2,1)} fusion(bf16[12576,768]{1,0:T(8,128)(2,1)} %param.7, s32[8192]{0:T(1024)S(1)} %broadcast_clamp_fusion), kind=kCustom, calls=%fused_computation | custom fusion | bytes 25198592 | tf_op jit(solution)/shard_map/jit(_take)/gather | solution.py:455
  57.9 19.8 %collective-permute-done = bf16[16,512,768]{2,1,0:T(8,128)(2,1)S(1)} collective-permute-done((bf16[16,512,768]{2,1,0:T(8,128)(2,1)S(1)}, bf16[16,512,768]{2,1,0:T(8,128)(2,1)S(1)}, u32[]{:S(2)}, u32[]{:S(2)}) %collective-permute-start) | collective-permute-done | bytes 12582944 | tf_op jit(solution)/shard_map/ppermute | solution.py:451
  82.8 151.4 %forward_pipe.1 = (bf16[16,512,768]{2,1,0:T(8,128)(2,1)}, bf16[16,512,768]{2,1,0:T(8,128)(2,1)}, bf16[16,512,768]{2,1,0:T(8,128)(2,1)}) custom-call(bf16[16,512,768]{2,1,0:T(8,128)(2,1)} %fusion.33.here_ref, bf16[768,3072]{1,0:T(8,128)(2,1)} %bitcast.79, bf16[3072,768]{1,0:T(8,128)(2,1)} %bitcast.78), custom_call_target="tpu_custom_call" | custom-call | flops 77309411328 | bytes 9437184 | tf_op jit(solution)/shard_map/forward_pipe/pallas_call | solution.py:131
  242.4 68.3 %collective-permute-done.3 = bf16[4,512,768]{2,1,0:T(8,128)(2,1)} collective-permute-done((bf16[4,512,768]{2,1,0:T(8,128)(2,1)}, bf16[4,512,768]{2,1,0:T(8,128)(2,1)}, u32[]{:S(2)}, u32[]{:S(2)}) %collective-permute-start.3) | collective-permute-done | bytes 3145760 | tf_op jit(solution)/shard_map/ppermute | solution.py:451
  330.1 23.8 %copy.43 = bf16[12576,768]{0,1:T(8,128)(2,1)} copy(bf16[12576,768]{1,0:T(8,128)(2,1)} %param.7) | data formatting | bytes 38633472 | tf_op args[2]
  356.3 26.0 %copy.72 = bf16[12576,768]{1,0:T(8,128)(2,1)} copy(bf16[12576,768]{0,1:T(8,128)(2,1)} %copy.43) | data formatting | bytes 38633472
  382.2 17.6 pad.4.clone.e_ref
  420.6 70.6 %head_fwd.4 = (bf16[4,12800,512]{2,1,0:T(8,128)(2,1)}, f32[4,5,5,512]{3,2,1,0:T(8,128)}, f32[4,3,512]{2,1,0:T(4,128)}) custom-call(bf16[4,768,512]{2,1,0:T(8,128)(2,1)} %copy.44.n_ref, bf16[12800,768]{1,0:T(8,128)(2,1)} %pad.4.clone.e_ref, s32[4,1,512]{2,1,0:T(1,128)} %copy.46.lab_ref), custom_call_target="tpu_custom_call" | custom-call | flops 40265318400 | bytes 72089600 | tf_op jit(solution)/shard_map/head_fwd/pallas_call | solution.py:332
  493.0 10.1 select_select_fusion.3
  516.0 70.6 %head_fwd.5 = (bf16[4,12800,512]{2,1,0:T(8,128)(2,1)}, f32[4,5,5,512]{3,2,1,0:T(8,128)}, f32[4,3,512]{2,1,0:T(4,128)}) custom-call(bf16[4,768,512]{2,1,0:T(8,128)(2,1)} %copy.47.n_ref, bf16[12800,768]{1,0:T(8,128)(2,1)} %pad.4.clone.e_ref, s32[4,1,512]{2,1,0:T(1,128)} %copy.49.lab_ref), custom_call_target="tpu_custom_call" | custom-call | flops 40265318400 | bytes 72089600 | tf_op jit(solution)/shard_map/head_fwd/pallas_call | solution.py:332
  586.6 70.7 %head_fwd.6 = (bf16[4,12800,512]{2,1,0:T(8,128)(2,1)}, f32[4,5,5,512]{3,2,1,0:T(8,128)}, f32[4,3,512]{2,1,0:T(4,128)}) custom-call(bf16[4,768,512]{2,1,0:T(8,128)(2,1)} %copy.50.n_ref, bf16[12800,768]{1,0:T(8,128)(2,1)} %pad.4.clone.e_ref, s32[4,1,512]{2,1,0:T(1,128)} %copy.52.lab_ref), custom_call_target="tpu_custom_call" | custom-call | flops 40265318400 | bytes 72089600 | tf_op jit(solution)/shard_map/head_fwd/pallas_call | solution.py:332
  657.3 70.7 %head_fwd.7 = (bf16[4,12800,512]{2,1,0:T(8,128)(2,1)}, f32[4,5,5,512]{3,2,1,0:T(8,128)}, f32[4,3,512]{2,1,0:T(4,128)}) custom-call(bf16[4,768,512]{2,1,0:T(8,128)(2,1)} %copy.53.n_ref, bf16[12800,768]{1,0:T(8,128)(2,1)} %pad.4.clone.e_ref, s32[4,1,512]{2,1,0:T(1,128)} %slice.121.lab_ref), custom_call_target="tpu_custom_call" | custom-call | flops 40265318400 | bytes 72089600 | tf_op jit(solution)/shard_map/head_fwd/pallas_call | solution.py:332
  728.9 16.1 all-gather
  749.9 65.2 %head_bwd.7 = (bf16[4,12800,512]{2,1,0:T(8,128)(2,1)}, bf16[4,512,768]{2,1,0:T(8,128)(2,1)}) custom-call(bf16[4,12800,512]{2,1,0:T(8,128)(2,1)} %get-tuple-element.47.p_ref, f32[4,5,5,512]{3,2,1,0:T(8,128)} %exponential_multiply_fusion.c_ref, s32[4,1,512]{2,1,0:T(1,128)} %slice.121.lab_ref, ...), custom_call_target="tpu_custom_call", output_to_operand_aliasing={{0}: (0, {})} | custom-call | flops 40265318400 | bytes 124518400 | tf_op jit(solution)/shard_map/head_bwd/pallas_call | solution.py:391
  817.4 65.1 %head_bwd.6 = (bf16[4,12800,512]{2,1,0:T(8,128)(2,1)}, bf16[4,512,768]{2,1,0:T(8,128)(2,1)}) custom-call(bf16[4,12800,512]{2,1,0:T(8,128)(2,1)} %get-tuple-element.44.p_ref, f32[4,5,5,512]{3,2,1,0:T(8,128)} %exponential_multiply_fusion.1.c_ref, s32[4,1,512]{2,1,0:T(1,128)} %copy.52.lab_ref, ...), custom_call_target="tpu_custom_call", output_to_operand_aliasing={{0}: (0, {})} | custom-call | flops 40265318400 | bytes 124518400 | tf_op jit(solution)/shard_map/head_bwd/pallas_call | solution.py:391
  886.2 65.2 %head_bwd.5 = (bf16[4,12800,512]{2,1,0:T(8,128)(2,1)}, bf16[4,512,768]{2,1,0:T(8,128)(2,1)}) custom-call(bf16[4,12800,512]{2,1,0:T(8,128)(2,1)} %get-tuple-element.41.p_ref, f32[4,5,5,512]{3,2,1,0:T(8,128)} %exponential_multiply_fusion.2.c_ref, s32[4,1,512]{2,1,0:T(1,128)} %copy.49.lab_ref, ...), custom_call_target="tpu_custom_call", output_to_operand_aliasing={{0}: (0, {})} | custom-call | flops 40265318400 | bytes 124518400 | tf_op jit(solution)/shard_map/head_bwd/pallas_call | solution.py:391
  955.1 65.5 %head_bwd.4 = (bf16[4,12800,512]{2,1,0:T(8,128)(2,1)}, bf16[4,512,768]{2,1,0:T(8,128)(2,1)}) custom-call(bf16[4,12800,512]{2,1,0:T(8,128)(2,1)} %get-tuple-element.37.p_ref, f32[4,5,5,512]{3,2,1,0:T(8,128)} %exponential_multiply_fusion.3.c_ref, s32[4,1,512]{2,1,0:T(1,128)} %copy.46.lab_ref, ...), custom_call_target="tpu_custom_call", output_to_operand_aliasing={{0}: (0, {})} | custom-call | flops 40265318400 | bytes 124518400 | tf_op jit(solution)/shard_map/head_bwd/pallas_call | solution.py:391
  1060.6 19.5 %fusion.2 = (f32[4,512]{1,0:T(4,128)S(1)}, f32[4,512]{1,0:T(4,128)S(1)}, f32[4,512]{1,0:T(4,128)S(1)}, f32[4,512]{1,0:T(4,128)S(1)}, f32[4,512]{1,0:T(4,128)S(1)...) fusion(bf16[16,512,768]{2,1,0:T(8,128)(2,1)} %get-tuple-element.40, bf16[4,512,768]{2,1,0:T(8,128)(2,1)} %collective-permute-done.14, ...), kind=kLoop, calls=%fused_computation.23 | loop fusion | flops 59754496 | bytes 50388992 | tf_op jit(solution)/shard_map/jvp()/reduce_sum | solution.py:30
  1080.4 12.3 fusion.4
  1102.3 308.5 %backward_pipe.1 = (bf16[16,512,768]{2,1,0:T(8,128)(2,1)}, bf16[16,512,3072]{2,1,0:T(8,128)(2,1)}, bf16[16,512,3072]{2,1,0:T(8,128)(2,1)}, bf16[16,512,768]{2,1,0:T(8,128)(2,1)}) custom-call(bf16[16,512,768]{2,1,0:T(8,128)(2,1)} %get-tuple-element.36.x_ref, bf16[16,512,768]{2,1,0:T(8,128)(2,1)} %pad_maximum_fusion.top_ref, bf16[768,3072]{1,0:T(8,128)(2,1)} %bitcast.80, ...), custom_call_target="tpu_custom_call" | custom-call | flops 115964116992 | bytes 9437184 | tf_op jit(solution)/shard_map/backward_pipe/pallas_call | solution.py:275
  1416.7 176.8 %table_grad.1 = f32[12576,768]{1,0:T(8,128)} custom-call(bf16[4,12800,512]{2,1,0:T(8,128)(2,1)} %get-tuple-element.53.refs_0_, bf16[4,12800,512]{2,1,0:T(8,128)(2,1)} %get-tuple-element.54.refs_1_, bf16[4,12800,512]{2,1,0:T(8,128)(2,1)} %get-tuple-element.55.refs_2_, bf16[4,12800,512]{2,1,0:T(8,128)(2,1)} %get-tuple-element.56.refs_3_, ...), custom_call_target="tpu_custom_call" | custom-call | flops 158242701312 | bytes 206045184 | tf_op jit(solution)/shard_map/table_grad/pallas_call | solution.py:425
  1594.1 48.3 %convolution_bitcast_fusion.1 = f32[1,768,3072]{2,1,0:T(8,128)} fusion(bf16[16,512,768]{2,1,0:T(8,128)(2,1)} %get-tuple-element.36.x_ref, bf16[16,512,3072]{2,1,0:T(8,128)(2,1)} %get-tuple-element.50), kind=kOutput, calls=%fused_computation.48 | convolution fusion | flops 38654705664 | bytes 72351744 | tf_op jit(solution)/shard_map/td,tf->df/dot_general | solution.py:507
  1642.5 49.0 %convolution_bitcast_fusion = f32[1,3072,768]{2,1,0:T(8,128)} fusion(bf16[16,512,3072]{2,1,0:T(8,128)(2,1)} %get-tuple-element.51, bf16[16,512,768]{2,1,0:T(8,128)(2,1)} %get-tuple-element.52), kind=kOutput, calls=%fused_computation.47 | convolution fusion | flops 38654705664 | bytes 72351744 | tf_op jit(solution)/shard_map/tf,td->fd/dot_general | solution.py:508
  1697.6 80.2 %scatter_custom_fusion = f32[12576,768]{1,0:T(8,128)} fusion(f32[12576,768]{1,0:T(8,128)} %table_grad.1, s32[8192]{0:T(1024)} %bitcast.87, bf16[8192,768]{1,0:T(8,128)(2,1)} %bitcast.71), kind=kCustom, calls=%fused_computation.2 | custom fusion | flops 12582912 | bytes 51216384 | tf_op jit(solution)/shard_map/scatter-add | solution.py:511
  (152 shorter events, 158.7 us)
Async XLA Ops:
  56.6 21.1 %collective-permute-start = (bf16[16,512,768]{2,1,0:T(8,128)(2,1)S(1)}, bf16[16,512,768]{2,1,0:T(8,128)(2,1)S(1)}, u32[]{:S(2)}, u32[]{:S(2)}) collective-permute-start(bf16[16,512,768]{2,1,0:T(8,128)(2,1)S(1)} %select_select_fusion), channel_id=1, source_target_pairs={{1,0},{3,2},{5,4},{7,6}} | collective-permute-start | bytes 37748744 | tf_op jit(solution)/shard_map/ppermute | solution.py:451
  236.3 4.6 collective-permute-start.2
  238.7 3.7 collective-permute-start.1
  240.9 69.8 %collective-permute-start.3 = (bf16[4,512,768]{2,1,0:T(8,128)(2,1)}, bf16[4,512,768]{2,1,0:T(8,128)(2,1)}, u32[]{:S(2)}, u32[]{:S(2)}) collective-permute-start(bf16[4,512,768]{2,1,0:T(8,128)(2,1)} %collective-permute-done.2), channel_id=1, source_target_pairs={{1,0},{5,4}} | collective-permute-start | bytes 9437192 | tf_op jit(solution)/shard_map/ppermute | solution.py:451
  320.3 95.6 %collective-permute-start.11 = (bf16[4,512,768]{2,1,0:T(8,128)(2,1)}, bf16[4,512,768]{2,1,0:T(8,128)(2,1)}, u32[]{:S(2)}, u32[]{:S(2)}) collective-permute-start(bf16[4,512,768]{2,1,0:T(8,128)(2,1)} %get-tuple-element.72), channel_id=1, source_target_pairs={{3,1},{7,5}} | collective-permute-start | bytes 9437192 | tf_op jit(solution)/shard_map/ppermute | solution.py:451
  322.9 93.8 %collective-permute-start.10 = (bf16[4,512,768]{2,1,0:T(8,128)(2,1)}, bf16[4,512,768]{2,1,0:T(8,128)(2,1)}, u32[]{:S(2)}, u32[]{:S(2)}) collective-permute-start(bf16[4,512,768]{2,1,0:T(8,128)(2,1)} %get-tuple-element.72), channel_id=1, source_target_pairs={{3,2},{7,6}} | collective-permute-start | bytes 9437192 | tf_op jit(solution)/shard_map/ppermute | solution.py:451
  325.2 92.8 %collective-permute-start.8 = (bf16[4,512,768]{2,1,0:T(8,128)(2,1)}, bf16[4,512,768]{2,1,0:T(8,128)(2,1)}, u32[]{:S(2)}, u32[]{:S(2)}) collective-permute-start(bf16[4,512,768]{2,1,0:T(8,128)(2,1)} %get-tuple-element.73), channel_id=1, source_target_pairs={{3,1},{7,5}} | collective-permute-start | bytes 9437192 | tf_op jit(solution)/shard_map/ppermute | solution.py:451
  327.6 91.7 %collective-permute-start.5 = (bf16[4,512,768]{2,1,0:T(8,128)(2,1)}, bf16[4,512,768]{2,1,0:T(8,128)(2,1)}, u32[]{:S(2)}, u32[]{:S(2)}) collective-permute-start(bf16[4,512,768]{2,1,0:T(8,128)(2,1)} %get-tuple-element.74), channel_id=1, source_target_pairs={{3,1},{7,5}} | collective-permute-start | bytes 9437192 | tf_op jit(solution)/shard_map/ppermute | solution.py:451
  410.7 80.6 %collective-permute-start.7 = (bf16[4,512,768]{2,1,0:T(8,128)(2,1)}, bf16[4,512,768]{2,1,0:T(8,128)(2,1)}, u32[]{:S(2)}, u32[]{:S(2)}) collective-permute-start(bf16[4,512,768]{2,1,0:T(8,128)(2,1)} %get-tuple-element.73), channel_id=1, source_target_pairs={{3,2},{7,6}} | collective-permute-start | bytes 9437192 | tf_op jit(solution)/shard_map/ppermute | solution.py:451
  415.9 75.4 %collective-permute-start.4 = (bf16[4,512,768]{2,1,0:T(8,128)(2,1)}, bf16[4,512,768]{2,1,0:T(8,128)(2,1)S(1)}, u32[]{:S(2)}, u32[]{:S(2)}) collective-permute-start(bf16[4,512,768]{2,1,0:T(8,128)(2,1)} %get-tuple-element.74), channel_id=1, source_target_pairs={{3,2},{7,6}} | collective-permute-start | bytes 9437192 | tf_op jit(solution)/shard_map/ppermute | solution.py:451
  416.7 74.6 %collective-permute-start.12 = (bf16[4,512,768]{2,1,0:T(8,128)(2,1)}, bf16[4,512,768]{2,1,0:T(8,128)(2,1)S(1)}, u32[]{:S(2)}, u32[]{:S(2)}) collective-permute-start(bf16[4,512,768]{2,1,0:T(8,128)(2,1)} %collective-permute-done.11), channel_id=1, source_target_pairs={{1,0},{5,4}} | collective-permute-start | bytes 9437192 | tf_op jit(solution)/shard_map/ppermute | solution.py:451
  418.0 73.3 %collective-permute-start.9 = (bf16[4,512,768]{2,1,0:T(8,128)(2,1)}, bf16[4,512,768]{2,1,0:T(8,128)(2,1)}, u32[]{:S(2)}, u32[]{:S(2)}) collective-permute-start(bf16[4,512,768]{2,1,0:T(8,128)(2,1)} %collective-permute-done.8), channel_id=1, source_target_pairs={{1,0},{5,4}} | collective-permute-start | bytes 9437192 | tf_op jit(solution)/shard_map/ppermute | solution.py:451
  419.3 73.6 %collective-permute-start.6 = (bf16[4,512,768]{2,1,0:T(8,128)(2,1)}, bf16[4,512,768]{2,1,0:T(8,128)(2,1)}, u32[]{:S(2)}, u32[]{:S(2)}) collective-permute-start(bf16[4,512,768]{2,1,0:T(8,128)(2,1)} %collective-permute-done.5), channel_id=1, source_target_pairs={{1,0},{5,4}} | collective-permute-start | bytes 9437192 | tf_op jit(solution)/shard_map/ppermute | solution.py:451
  815.1 207.3 %collective-permute-start.19 = (bf16[4,512,768]{2,1,0:T(8,128)(2,1)}, bf16[4,512,768]{2,1,0:T(8,128)(2,1)S(1)}, u32[]{:S(2)}, u32[]{:S(2)}) collective-permute-start(bf16[4,512,768]{2,1,0:T(8,128)(2,1)} %get-tuple-element.49), channel_id=1, source_target_pairs={{0,1},{2,3},{4,5},{6,7}} | collective-permute-start | bytes 9437192 | tf_op jit(solution)/shard_map/ppermute | solution.py:451
  882.5 145.1 %collective-permute-start.17 = (bf16[4,512,768]{2,1,0:T(8,128)(2,1)}, bf16[4,512,768]{2,1,0:T(8,128)(2,1)}, u32[]{:S(2)}, u32[]{:S(2)}) collective-permute-start(bf16[4,512,768]{2,1,0:T(8,128)(2,1)} %get-tuple-element.46), channel_id=1, source_target_pairs={{0,1},{2,3},{4,5},{6,7}} | collective-permute-start | bytes 9437192 | tf_op jit(solution)/shard_map/ppermute | solution.py:451
  951.4 83.1 %collective-permute-start.15 = (bf16[4,512,768]{2,1,0:T(8,128)(2,1)}, bf16[4,512,768]{2,1,0:T(8,128)(2,1)}, u32[]{:S(2)}, u32[]{:S(2)}) collective-permute-start(bf16[4,512,768]{2,1,0:T(8,128)(2,1)} %get-tuple-element.43), channel_id=1, source_target_pairs={{0,1},{2,3},{4,5},{6,7}} | collective-permute-start | bytes 9437192 | tf_op jit(solution)/shard_map/ppermute | solution.py:451
  1020.7 19.2 %collective-permute-start.13 = (bf16[4,512,768]{2,1,0:T(8,128)(2,1)}, bf16[4,512,768]{2,1,0:T(8,128)(2,1)S(1)}, u32[]{:S(2)}, u32[]{:S(2)}) collective-permute-start(bf16[4,512,768]{2,1,0:T(8,128)(2,1)} %get-tuple-element.39), channel_id=1, source_target_pairs={{0,1},{2,3},{4,5},{6,7}} | collective-permute-start | bytes 9437192 | tf_op jit(solution)/shard_map/ppermute | solution.py:451
  1025.1 33.8 %collective-permute-start.20 = (bf16[4,512,768]{2,1,0:T(8,128)(2,1)}, bf16[4,512,768]{2,1,0:T(8,128)(2,1)}, u32[]{:S(2)}, u32[]{:S(2)}) collective-permute-start(bf16[4,512,768]{2,1,0:T(8,128)(2,1)} %fusion.17), channel_id=1, source_target_pairs={{1,3},{5,7}} | collective-permute-start | bytes 9437192 | tf_op jit(solution)/shard_map/ppermute | solution.py:451
  1032.0 26.9 %collective-permute-start.18 = (bf16[4,512,768]{2,1,0:T(8,128)(2,1)}, bf16[4,512,768]{2,1,0:T(8,128)(2,1)}, u32[]{:S(2)}, u32[]{:S(2)}) collective-permute-start(bf16[4,512,768]{2,1,0:T(8,128)(2,1)} %fusion.16), channel_id=1, source_target_pairs={{1,3},{5,7}} | collective-permute-start | bytes 9437192 | tf_op jit(solution)/shard_map/ppermute | solution.py:451
  1039.0 19.9 %collective-permute-start.16 = (bf16[4,512,768]{2,1,0:T(8,128)(2,1)}, bf16[4,512,768]{2,1,0:T(8,128)(2,1)S(1)}, u32[]{:S(2)}, u32[]{:S(2)}) collective-permute-start(bf16[4,512,768]{2,1,0:T(8,128)(2,1)} %fusion.15), channel_id=1, source_target_pairs={{1,3},{5,7}} | collective-permute-start | bytes 9437192 | tf_op jit(solution)/shard_map/ppermute | solution.py:451
  1042.5 18.1 %collective-permute-start.14 = (bf16[4,512,768]{2,1,0:T(8,128)(2,1)}, bf16[4,512,768]{2,1,0:T(8,128)(2,1)}, u32[]{:S(2)}, u32[]{:S(2)}) collective-permute-start(bf16[4,512,768]{2,1,0:T(8,128)(2,1)} %fusion.14), channel_id=1, source_target_pairs={{1,3},{5,7}} | collective-permute-start | bytes 9437192 | tf_op jit(solution)/shard_map/ppermute | solution.py:451
  1410.9 280.6 %collective-permute-start.21 = (bf16[16,512,768]{2,1,0:T(8,128)(2,1)}, bf16[16,512,768]{2,1,0:T(8,128)(2,1)}, u32[]{:S(2)}, u32[]{:S(2)}) collective-permute-start(bf16[16,512,768]{2,1,0:T(8,128)(2,1)} %get-tuple-element.57), channel_id=1, source_target_pairs={{0,1},{2,3},{4,5},{6,7}} | collective-permute-start | bytes 37748744 | tf_op jit(solution)/shard_map/ppermute | solution.py:451
  1594.1 97.3 %slice-start.6 = ((s8[12582912]{0:T(1024)(128)(4,1)}), s8[4194304]{0:T(1024)(128)(4,1)S(1)}, s32[]{:S(2)}) async-start(s8[12582912]{0:T(1024)(128)(4,1)} %bitcast.72), calls=%async_computation.6 | async-start | bytes 8388608
  1594.1 97.3 %slice-start.7 = ((s8[12582912]{0:T(1024)(128)(4,1)}), s8[4194304]{0:T(1024)(128)(4,1)S(1)}, s32[]{:S(2)}) async-start(s8[12582912]{0:T(1024)(128)(4,1)} %bitcast.72), calls=%async_computation.7 | async-start | bytes 8388608
  (27 other events, 884.1 us)

commit v3 on v2

--- a/solution.py
+++ b/solution.py
@@ -7,17 +7,15 @@
 from jax.sharding import PartitionSpec as P
 
 NORM_EPS = 1e-6
-LOG2E = 1.4426950408889634
-LN2 = 0.6931471805599453
 GELU_K = 0.7978845608028654
 GELU_A = 0.044715
-SUB = 512
-SUBS = 5
+SUB = 256
+SUBS = 10
 STAGES = 4
 MESH = pl.DeviceIdType.MESH
 PIPE_CAP = 60 * 1024 * 1024
 TILE = SUB * SUBS
-GROUPS = 4
+CUTS = (0, 2, 6, 11, 16)
 PARTS = 6
 V_TILE = 640
 VMEM_CAP = 56 * 1024 * 1024
@@ -83,9 +81,13 @@
         pltpu.make_async_copy(recv.at[m], save_ref.at[m], save_sem.at[m]).start()
         x = recv[m]
         total = None
+        ahead = jnp.dot(x, w1[:, 0:width], preferred_element_type=F32)
         for part in range(PARTS):
             cols = slice(part * width, (part + 1) * width)
-            hidden = gelu_hidden(jnp.dot(x, w1[:, cols], preferred_element_type=F32))
+            pre = ahead
+            if part < PARTS - 1:
+                ahead = jnp.dot(x, w1[:, (part + 1) * width:(part + 2) * width], preferred_element_type=F32)
+            hidden = gelu_hidden(pre)
             term = jnp.dot(hidden, w2[cols, :], preferred_element_type=F32)
             total = term if total is None else total + term
         out_buf[m] = (x.astype(F32) + total).astype(BF)
@@ -222,11 +224,19 @@
 
         x = x_buf[slot]
         grad_out = recv[m]
+
+        def both(part):
+            cols = slice(part * width, (part + 1) * width)
+            return (jnp.dot(x, w1[:, cols], preferred_element_type=F32),
+                    jnp.dot(grad_out, w2t[:, cols], preferred_element_type=F32))
+
         total = None
+        ahead = both(0)
         for part in range(PARTS):
             cols = slice(part * width, (part + 1) * width)
-            pre = jnp.dot(x, w1[:, cols], preferred_element_type=F32)
-            grad_hidden = jnp.dot(grad_out, w2t[:, cols], preferred_element_type=F32)
+            pre, grad_hidden = ahead
+            if part < PARTS - 1:
+                ahead = both(part + 1)
             sq = pre * pre
             inner = jnp.tanh(pre * (GELU_K + (GELU_K * GELU_A) * sq))
             side = 0.5 + 0.5 * inner
@@ -292,7 +302,7 @@
     )(saved_in, grad_last, w1, w1t, w2t)
 
 
-def head_forward_body(n_valid, log_scale, n_ref, e_ref, lab_ref, p_ref, m_ref, st_ref, run):
+def head_forward_body(n_valid, scale, n_ref, e_ref, lab_ref, p_ref, m_ref, st_ref, run):
     tile, chunk = pl.program_id(0), pl.program_id(1)
 
     @pl.when(tile == 0)
@@ -306,13 +316,13 @@
     rows = lax.broadcasted_iota(jnp.int32, (SUB, n_rows.shape[1]), 0)
     for sub in range(SUBS):
         cut = slice(sub * SUB, (sub + 1) * SUB)
-        logit = jnp.dot(e_ref[cut, :], n_rows, preferred_element_type=F32) * log_scale
+        logit = jnp.dot(e_ref[cut, :], n_rows, preferred_element_type=F32) * scale
         if sub == SUBS - 1:
             logit = jnp.where(rows < n_valid - tile * TILE - sub * SUB, logit, -jnp.inf)
         hit = hit + jnp.sum(jnp.where(rows == lab - sub * SUB, logit, 0.0), axis=0, keepdims=True)
         new_top = jnp.maximum(top, jnp.max(logit, axis=0, keepdims=True))
-        expo = jnp.exp2(logit - new_top)
-        tot = tot * jnp.exp2(top - new_top) + jnp.sum(expo, axis=0, keepdims=True)
+        expo = jnp.exp(logit - new_top)
+        tot = tot * jnp.exp(top - new_top) + jnp.sum(expo, axis=0, keepdims=True)
         p_ref[0, cut, :] = expo.astype(BF)
         m_ref[0, 0, sub:sub + 1, :] = new_top
         top = new_top
@@ -324,13 +334,33 @@
     st_ref[0, 2:3, :] = hit
 
 
-def head_forward(normed, emb_pad, labels, n_valid, log_scale):
+def transpose_body(n_valid, e_ref, out_ref):
+    rows = lax.broadcasted_iota(jnp.int32, e_ref.shape, 0)
+    out_ref[...] = jnp.where(rows < n_valid - pl.program_id(0) * e_ref.shape[0], e_ref[...], 0).T
+
+
+def transposed_table(emb_rows, padded, width=1280):
+    n_valid, dim = emb_rows.shape
+    return pl.pallas_call(
+        functools.partial(transpose_body, n_valid),
+        grid=(padded // width,),
+        in_specs=[pl.BlockSpec((width, dim), lambda t: (t, 0))],
+        out_specs=pl.BlockSpec((dim, width), lambda t: (0, t)),
+        out_shape=jax.ShapeDtypeStruct((dim, padded), BF),
+        compiler_params=pltpu.CompilerParams(vmem_limit_bytes=VMEM_CAP),
+        cost_estimate=pl.CostEstimate(flops=20 * padded * dim, bytes_accessed=4 * padded * dim, transcendentals=0),
+        name="table_t",
+    )(emb_rows)
+
+
+def head_forward(normed, emb_rows, labels, scale):
     chunks, dim, rows = normed.shape
-    padded = emb_pad.shape[0]
-    tiles = padded // TILE
+    n_valid = emb_rows.shape[0]
+    tiles = -(-n_valid // TILE)
+    padded = tiles * TILE
     row = pl.BlockSpec((1, 1, rows), lambda t, c: (c, 0, 0))
     return pl.pallas_call(
-        functools.partial(head_forward_body, n_valid, log_scale),
+        functools.partial(head_forward_body, n_valid, scale),
         grid=(tiles, chunks),
         in_specs=[
             pl.BlockSpec((1, dim, rows), lambda t, c: (c, 0, 0)),
@@ -351,7 +381,7 @@
         compiler_params=pltpu.CompilerParams(vmem_limit_bytes=VMEM_CAP),
         cost_estimate=pl.CostEstimate(flops=2 * chunks * rows * dim * padded, bytes_accessed=padded * (2 * dim + 2 * rows * chunks), transcendentals=rows * chunks * padded),
         name="head_fwd",
-    )(normed, emb_pad, labels)
+    )(normed, emb_rows, labels)
 
 
 def head_backward_body(p_ref, c_ref, lab_ref, g_ref, et_ref, d_ref, out_ref, acc_ref):
@@ -359,13 +389,20 @@
     lab = lab_ref[0] - tile * TILE
     gain = g_ref[0]
     rows = lax.broadcasted_iota(jnp.int32, (SUB, lab.shape[1]), 0)
-    total = None
-    for sub in range(SUBS):
+    def delta_of(sub):
         cut = slice(sub * SUB, (sub + 1) * SUB)
         prob = p_ref[0, cut, :].astype(F32) * c_ref[0, 0, sub:sub + 1, :]
         delta = jnp.where(rows == lab - sub * SUB, gain, prob).astype(BF)
         d_ref[0, cut, :] = delta
-        term = jnp.dot(et_ref[:, cut], delta, preferred_element_type=F32)
+        return delta
+
+    total = None
+    ahead = delta_of(0)
+    for sub in range(SUBS):
+        delta = ahead
+        if sub < SUBS - 1:
+            ahead = delta_of(sub + 1)
+        term = jnp.dot(et_ref[:, sub * SUB:(sub + 1) * SUB], delta, preferred_element_type=F32)
         total = term if total is None else total + term
 
     @pl.when(tile == 0)
@@ -419,14 +456,14 @@
 
 
 def table_grad(deltas, normed, slice_rows, v_tile):
-    chunks, rows, dim = normed[0].shape
+    _, rows, dim = normed[0].shape
     groups = len(deltas)
-    tokens = groups * chunks * rows
+    tokens = sum(part.shape[0] for part in normed) * rows
     return pl.pallas_call(
         functools.partial(table_grad_body, groups),
         grid=(-(-slice_rows // v_tile),),
-        in_specs=[pl.BlockSpec((chunks, v_tile, rows), lambda v: (0, v, 0))] * groups
-        + [pl.BlockSpec((chunks, rows, dim), lambda v: (0, 0, 0), pipeline_mode=pl.Buffered(1))] * groups,
+        in_specs=[pl.BlockSpec((part.shape[0], v_tile, rows), lambda v: (0, v, 0)) for part in deltas]
+        + [pl.BlockSpec(part.shape, lambda v: (0, 0, 0), pipeline_mode=pl.Buffered(1)) for part in normed],
         out_specs=pl.BlockSpec((v_tile, dim), lambda v: (v, 0)),
         out_shape=jax.ShapeDtypeStruct((slice_rows, dim), F32),
         compiler_params=pltpu.CompilerParams(vmem_limit_bytes=VMEM_CAP),
@@ -445,7 +482,7 @@
         w1, w2 = w_in[0], w_out[0]
         row_start = stage * slice_rows
         padded = -(-slice_rows // TILE) * TILE
-        per = micro_count // GROUPS
+        unit = micro_count // CUTS[-1]
 
         def hop(value, *pairs):
             return lax.ppermute(value, "stage", pairs)
@@ -456,48 +493,55 @@
         own_rows = jnp.where(tok_here[..., None], looked_up, 0)
         chip_rows = own_rows + hop(own_rows, (1, 0), (3, 2))
 
-        emb_pad = jnp.pad(emb_rows, ((0, padded - slice_rows), (0, 0)))
-        emb_t = emb_pad.T
+        emb_t = transposed_table(emb_rows, padded)
         local_lab = label_ids - row_start
         labels = jnp.where((local_lab >= 0) & (local_lab < slice_rows), local_lab, -1)[:, None]
 
         saved_in, last_out, normed = forward_pipe(chip_rows, w1, w2)
 
-        cuts = [slice(g * per, (g + 1) * per) for g in range(GROUPS)]
+        cuts = [slice(lo * unit, hi * unit) for lo, hi in zip(CUTS[:-1], CUTS[1:])]
         n_parts, expo, maxes, stats = [], [], [], []
-        for cut in cuts:
+        for g, cut in enumerate(cuts):
             own = normed[cut]
+            if g > 0:
+                own, n_parts[-1] = lax.optimization_barrier((own, n_parts[-1]))
             near = hop(own, (3, 2))
             cross = hop(own, (3, 1))
-            final = hop(cross, (1, 0))
-            part = jnp.where(stage == 3, own, jnp.where(stage == 2, near, jnp.where(stage == 1, cross, final)))
+            relay = cross
+            if g > 0:
+                relay, stats[-1] = lax.optimization_barrier((cross, stats[-1]))
+            final = hop(relay, (1, 0))
+            part = jnp.where(stage == 3, own, jnp.where(stage == 2, near, jnp.where(stage == 1, relay, final)))
+            res = head_forward(part.transpose(0, 2, 1), emb_rows, labels[cut], scale)
             n_parts.append(part)
-            res = head_forward(part.transpose(0, 2, 1), emb_pad, labels[cut], slice_rows, scale * LOG2E)
             expo.append(res[0])
             maxes.append(res[1])
             stats.append(res[2])
 
         every = lax.all_gather(jnp.concatenate(stats), "stage")
         top = jnp.max(every[:, :, 0], axis=0)
-        denom = jnp.sum(every[:, :, 1] * jnp.exp2(every[:, :, 0] - top), axis=0)
+        denom = jnp.sum(every[:, :, 1] * jnp.exp(every[:, :, 0] - top), axis=0)
         hit = jnp.sum(every[:, :, 2], axis=0)
-        mean_loss = (jnp.sum(jnp.log2(denom) + top - hit) * (LN2 / (micro_count * micro_tokens))).reshape(1)
+        mean_loss = (jnp.sum(jnp.log(denom) + top - hit) / (micro_count * micro_tokens)).reshape(1)
         ratio = scale / denom
-        gain = ((jnp.exp2(hit - top) / denom - 1.0) * scale)[:, None]
-
-        deltas, grad_last = [], []
+        gain = ((jnp.exp(hit - top) / denom - 1.0) * scale)[:, None]
+
+        deltas, pairs = [], []
         for g, cut in enumerate(cuts):
-            coef = jnp.exp2(maxes[g] - top[cut, None, None]) * ratio[cut, None, None]
+            coef = jnp.exp(maxes[g] - top[cut, None, None]) * ratio[cut, None, None]
             delta, part = head_backward(expo[g], coef, labels[cut], gain[cut], emb_t)
+            if g >= 2:
+                part, pairs[g - 2] = lax.optimization_barrier((part, pairs[g - 2]))
             deltas.append(delta)
-            near = hop(part, (0, 1), (2, 3)).astype(F32)
-            pair = part.astype(F32) + near
-            far = hop(pair.astype(BF), (1, 3)).astype(F32)
-            _, pull = jax.vjp(norm_f32, last_out[cut])
-            grad_last.append(pull(pair + far)[0])
-        grad_last = jnp.concatenate(grad_last)
-
+            pairs.append(part.astype(F32) + hop(part, (0, 1), (2, 3)).astype(F32))
+        sent = [pair.astype(BF) for pair in pairs]
+        deltas, sent, pairs = lax.optimization_barrier((deltas, sent, pairs))
+        far = [hop(value, (1, 3)) for value in sent]
         grad_head = table_grad(deltas, n_parts, slice_rows, V_TILE)
+        far, grad_head = lax.optimization_barrier((far, grad_head))
+        grad_n = jnp.concatenate([pair + value.astype(F32) for pair, value in zip(pairs, far)])
+        _, pull = jax.vjp(norm_f32, last_out)
+        grad_last = pull(grad_n)[0]
 
         grads, hidden, grad_pre, dx_rows = backward_pipe(saved_in, grad_last, w1, w1.T, w2.T)
 

time: 1800 us -> 1650 us (0.917)
  Pallas kernels: 1180 us -> 1100 us
  local copies, waits for them, and re-layouts: 164 us -> 92.7 us
    pallas_call x1, Pallas kernels: 309 us -> 203 us  [backward_pipe(): pl.pallas_call(backward_pipe_body, in_specs=[any_spec] * 5, out_specs=[an...]
    unnamed x64 -> x54, local copies, waits for them, and re-layouts: 68.7 us -> 13.4 us
    add x0 -> x8, other arithmetic: none -> 48 us  [the longest x4 24.7 us: stage_body(): pair + value.astype(F32)]
    pallas_call x4 -> x5, Pallas kernels: 283 us -> 310 us  [the longest x4 292 us: head_forward(): pl.pallas_call(functools.partial(head_forward_body, n_valid, scale), grid...]
  transfers between devices with their start and end apart: 22 -> 22, of which waited for: 2 -> 4; matrix products, arithmetic and copies ran while one was open for 12% -> 10% of each run, Pallas kernels for 25% -> 38%
where the time goes in v3:
time: 1650 us; the launch traced here: 1630 us
  Pallas kernels  1100 us (67%)
  other arithmetic  199 us (12%)
  matrix products  97 us (6%)
  local copies, waits for them, and re-layouts  92.7 us (6%)
  waiting for transfers between devices  74.2 us (4%)
  starting transfers between devices  53.7 us (3%)
    pallas_call x4, Pallas kernels, head_forward(): pl.pallas_call(functools.partial(head_forward_body, n_valid, scale), grid...  292 us
    pallas_call x4, Pallas kernels, head_backward(): pl.pallas_call(head_backward_body, grid=(tiles, chunks), in_specs=[block,...  260 us
    pallas_call x1, Pallas kernels, backward_pipe(): pl.pallas_call(backward_pipe_body, in_specs=[any_spec] * 5, out_specs=[an...  203 us
    pallas_call x1, Pallas kernels, table_grad(): pl.pallas_call(functools.partial(table_grad_body, groups), grid=(-(-slice...  177 us
    pallas_call x1, Pallas kernels, forward_pipe(): pl.pallas_call(forward_pipe_body, in_specs=[any_spec] * 3, out_specs=[any...  151 us
    scatter-add x1, other arithmetic, stage_body(): grad_head.at[seg].add(dx_rows.reshape(-1, dim).astype(F32), mode='drop')  80.5 us
    ppermute x22, waiting for transfers between devices, hop(): return lax.ppermute(value, 'stage', pairs)  74.2 us
    ppermute x22, starting transfers between devices, hop(): return lax.ppermute(value, 'stage', pairs)  53.7 us
  transfers between devices with their start and end apart: 22, of which 4 were waited for; matrix products, arithmetic and copies ran while one was open for 10% of the time, Pallas kernels for 38%

profile of v3, /device:TPU:0, one launch (start us, length us, event | category | flops | bytes accessed | tf_op | source)
XLA Modules:
  0.0 1633.9 jit_solution(14906122533849421908)
XLA Ops:
  2.8 46.0 %gather_fusion = bf16[8192,768]{1,0:T(8,128)(2,1)} fusion(bf16[12576,768]{1,0:T(8,128)(2,1)} %e_ref.9, s32[8192]{0:T(1024)S(1)} %broadcast_clamp_fusion), kind=kCustom, calls=%fused_computation | custom fusion | bytes 25198592 | tf_op jit(solution)/shard_map/jit(_take)/gather | solution.py:492
  57.9 19.8 %collective-permute-done = bf16[16,512,768]{2,1,0:T(8,128)(2,1)S(1)} collective-permute-done((bf16[16,512,768]{2,1,0:T(8,128)(2,1)S(1)}, bf16[16,512,768]{2,1,0:T(8,128)(2,1)S(1)}, u32[]{:S(2)}, u32[]{:S(2)}) %collective-permute-start) | collective-permute-done | bytes 12582944 | tf_op jit(solution)/shard_map/ppermute | solution.py:488
  82.8 151.0 %forward_pipe.1 = (bf16[16,512,768]{2,1,0:T(8,128)(2,1)}, bf16[16,512,768]{2,1,0:T(8,128)(2,1)}, bf16[16,512,768]{2,1,0:T(8,128)(2,1)}) custom-call(bf16[16,512,768]{2,1,0:T(8,128)(2,1)} %fusion.21.here_ref, bf16[768,3072]{1,0:T(8,128)(2,1)} %bitcast.73, bf16[3072,768]{1,0:T(8,128)(2,1)} %bitcast.72), custom_call_target="tpu_custom_call" | custom-call | flops 77309411328 | bytes 9437184 | tf_op jit(solution)/shard_map/forward_pipe/pallas_call | solution.py:133
  243.7 47.0 %collective-permute-done.3 = bf16[2,512,768]{2,1,0:T(8,128)(2,1)} collective-permute-done((bf16[2,512,768]{2,1,0:T(8,128)(2,1)}, bf16[2,512,768]{2,1,0:T(8,128)(2,1)}, u32[]{:S(2)}, u32[]{:S(2)}) %collective-permute-start.3) | collective-permute-done | bytes 1572896 | tf_op jit(solution)/shard_map/ppermute | solution.py:488
  301.8 38.5 %head_fwd.4 = (bf16[2,12800,512]{2,1,0:T(8,128)(2,1)}, f32[2,5,10,512]{3,2,1,0:T(8,128)}, f32[2,3,512]{2,1,0:T(4,128)}) custom-call(bf16[2,768,512]{2,1,0:T(8,128)(2,1)} %copy.38.n_ref, bf16[12576,768]{1,0:T(8,128)(2,1)} %e_ref.9, s32[2,1,512]{2,1,0:T(1,128)} %copy.39.lab_ref), custom_call_target="tpu_custom_call" | custom-call | flops 20132659200 | bytes 45875200 | tf_op jit(solution)/shard_map/head_fwd/pallas_call | solution.py:362
  357.9 73.0 %head_fwd.5 = (bf16[4,12800,512]{2,1,0:T(8,128)(2,1)}, f32[4,5,10,512]{3,2,1,0:T(8,128)}, f32[4,3,512]{2,1,0:T(4,128)}) custom-call(bf16[4,768,512]{2,1,0:T(8,128)(2,1)} %copy.40.n_ref, bf16[12576,768]{1,0:T(8,128)(2,1)} %e_ref.9, s32[4,1,512]{2,1,0:T(1,128)} %copy.41.lab_ref), custom_call_target="tpu_custom_call" | custom-call | flops 40265318400 | bytes 72089600 | tf_op jit(solution)/shard_map/head_fwd/pallas_call | solution.py:362
  454.3 90.3 %head_fwd.6 = (bf16[5,12800,512]{2,1,0:T(8,128)(2,1)}, f32[5,5,10,512]{3,2,1,0:T(8,128)}, f32[5,3,512]{2,1,0:T(4,128)}) custom-call(bf16[5,768,512]{2,1,0:T(8,128)(2,1)} %copy.42.n_ref, bf16[12576,768]{1,0:T(8,128)(2,1)} %e_ref.9, s32[5,1,512]{2,1,0:T(1,128)} %copy.43.lab_ref), custom_call_target="tpu_custom_call" | custom-call | flops 50331648000 | bytes 85196800 | tf_op jit(solution)/shard_map/head_fwd/pallas_call | solution.py:362
  546.6 18.2 %table_t.1.et_ref = bf16[768,12800]{1,0:T(8,128)(2,1)} custom-call(bf16[12576,768]{1,0:T(8,128)(2,1)} %e_ref.9), custom_call_target="tpu_custom_call" | custom-call | flops 196608000 | bytes 39321600 | tf_op jit(solution)/shard_map/table_t/pallas_call | solution.py:344
  573.6 90.4 %head_fwd.7 = (bf16[5,12800,512]{2,1,0:T(8,128)(2,1)}, f32[5,5,10,512]{3,2,1,0:T(8,128)}, f32[5,3,512]{2,1,0:T(4,128)}) custom-call(bf16[5,768,512]{2,1,0:T(8,128)(2,1)} %copy.44.n_ref, bf16[12576,768]{1,0:T(8,128)(2,1)} %e_ref.9, s32[5,1,512]{2,1,0:T(1,128)} %slice.109.lab_ref), custom_call_target="tpu_custom_call" | custom-call | flops 50331648000 | bytes 85196800 | tf_op jit(solution)/shard_map/head_fwd/pallas_call | solution.py:362
  664.9 12.5 all-gather
  681.4 39.3 %head_bwd.4 = (bf16[2,12800,512]{2,1,0:T(8,128)(2,1)}, bf16[2,512,768]{2,1,0:T(8,128)(2,1)}) custom-call(bf16[2,12800,512]{2,1,0:T(8,128)(2,1)} %get-tuple-element.79.p_ref, f32[2,5,10,512]{3,2,1,0:T(8,128)} %exponential_multiply_fusion.3.c_ref, s32[2,1,512]{2,1,0:T(1,128)} %copy.39.lab_ref, ...), custom_call_target="tpu_custom_call", output_to_operand_aliasing={{0}: (0, {})} | custom-call | flops 20132659200 | bytes 72089600 | tf_op jit(solution)/shard_map/head_bwd/pallas_call | solution.py:428
  724.4 65.1 %head_bwd.5 = (bf16[4,12800,512]{2,1,0:T(8,128)(2,1)}, bf16[4,512,768]{2,1,0:T(8,128)(2,1)}) custom-call(bf16[4,12800,512]{2,1,0:T(8,128)(2,1)} %get-tuple-element.82.p_ref, f32[4,5,10,512]{3,2,1,0:T(8,128)} %exponential_multiply_fusion.2.c_ref, s32[4,1,512]{2,1,0:T(1,128)} %copy.41.lab_ref, ...), custom_call_target="tpu_custom_call", output_to_operand_aliasing={{0}: (0, {})} | custom-call | flops 40265318400 | bytes 124518400 | tf_op jit(solution)/shard_map/head_bwd/pallas_call | solution.py:428
  793.5 77.7 %head_bwd.6 = (bf16[5,12800,512]{2,1,0:T(8,128)(2,1)}, bf16[5,512,768]{2,1,0:T(8,128)(2,1)}) custom-call(bf16[5,12800,512]{2,1,0:T(8,128)(2,1)} %get-tuple-element.85.p_ref, f32[5,5,10,512]{3,2,1,0:T(8,128)} %exponential_multiply_fusion.1.c_ref, s32[5,1,512]{2,1,0:T(1,128)} %copy.43.lab_ref, ...), custom_call_target="tpu_custom_call", output_to_operand_aliasing={{0}: (0, {})} | custom-call | flops 50331648000 | bytes 150732800 | tf_op jit(solution)/shard_map/head_bwd/pallas_call | solution.py:428
  875.8 77.5 %head_bwd.7 = (bf16[5,12800,512]{2,1,0:T(8,128)(2,1)}, bf16[5,512,768]{2,1,0:T(8,128)(2,1)}) custom-call(bf16[5,12800,512]{2,1,0:T(8,128)(2,1)} %get-tuple-element.88.p_ref, f32[5,5,10,512]{3,2,1,0:T(8,128)} %exponential_multiply_fusion.c_ref, s32[5,1,512]{2,1,0:T(1,128)} %slice.109.lab_ref, ...), custom_call_target="tpu_custom_call", output_to_operand_aliasing={{0}: (0, {})} | custom-call | flops 50331648000 | bytes 150732800 | tf_op jit(solution)/shard_map/head_bwd/pallas_call | solution.py:428
  981.2 8.9 convert_add_fusion.3
  990.0 8.9 convert_add_fusion.2
  1008.4 176.7 %table_grad.1 = f32[12576,768]{1,0:T(8,128)} custom-call(bf16[2,12800,512]{2,1,0:T(8,128)(2,1)} %get-tuple-element.104.refs_0_, bf16[4,12800,512]{2,1,0:T(8,128)(2,1)} %get-tuple-element.105.refs_1_, bf16[5,12800,512]{2,1,0:T(8,128)(2,1)} %get-tuple-element.106.refs_2_, bf16[5,12800,512]{2,1,0:T(8,128)(2,1)} %get-tuple-element.107.refs_3_, ...), custom_call_target="tpu_custom_call" | custom-call | flops 158242701312 | bytes 206045184 | tf_op jit(solution)/shard_map/table_grad/pallas_call | solution.py:462
  1188.0 8.0 convert_add_fusion.1
  1209.9 10.4 fusion
  1220.4 18.2 %fusion.2.top_ref = bf16[16,512,768]{2,1,0:T(8,128)(2,1)} fusion(bf16[16,512,768]{2,1,0:T(8,128)(2,1)} %get-tuple-element.118, f32[5,512,768]{2,1,0:T(8,128)} %copy-done, f32[5,512,768]{2,1,0:T(8,128)} %copy-done.1, f32[4,512,768]{2,1,0:T(8,128)} %copy-done.2, f32[2,512,768]{2,1,0:T(8,128)} %convert_add_fusion.6, f32[16,512]{1,0:T(8,128)S(1)} %get-tuple-element.139, ...), kind=kLoop, calls=%fused_computation.8 | loop fusion | flops 56623104 | bytes 50397184 | tf_op jit(solution)/shard_map/transpose(jvp())/convert_element_type | solution.py:27
  1238.5 203.1 %backward_pipe.1 = (bf16[16,512,768]{2,1,0:T(8,128)(2,1)}, bf16[16,512,3072]{2,1,0:T(8,128)(2,1)}, bf16[16,512,3072]{2,1,0:T(8,128)(2,1)}, bf16[16,512,768]{2,1,0:T(8,128)(2,1)}) custom-call(bf16[16,512,768]{2,1,0:T(8,128)(2,1)} %get-tuple-element.78.x_ref, bf16[16,512,768]{2,1,0:T(8,128)(2,1)} %fusion.2.top_ref, bf16[768,3072]{1,0:T(8,128)(2,1)} %bitcast.74, ...), custom_call_target="tpu_custom_call" | custom-call | flops 115964116992 | bytes 9437184 | tf_op jit(solution)/shard_map/backward_pipe/pallas_call | solution.py:285
  1448.5 48.3 %convolution_bitcast_fusion.1 = f32[1,768,3072]{2,1,0:T(8,128)} fusion(bf16[16,512,768]{2,1,0:T(8,128)(2,1)} %get-tuple-element.78.x_ref, bf16[16,512,3072]{2,1,0:T(8,128)(2,1)} %get-tuple-element.119), kind=kOutput, calls=%fused_computation.21 | convolution fusion | flops 38654705664 | bytes 72351744 | tf_op jit(solution)/shard_map/td,tf->df/dot_general | solution.py:551
  1496.8 48.7 %convolution_bitcast_fusion = f32[1,3072,768]{2,1,0:T(8,128)} fusion(bf16[16,512,3072]{2,1,0:T(8,128)(2,1)} %get-tuple-element.120, bf16[16,512,768]{2,1,0:T(8,128)(2,1)} %get-tuple-element.121), kind=kOutput, calls=%fused_computation.20 | convolution fusion | flops 38654705664 | bytes 72351744 | tf_op jit(solution)/shard_map/tf,td->fd/dot_general | solution.py:552
  1551.8 80.5 %scatter_custom_fusion = f32[12576,768]{1,0:T(8,128)} fusion(f32[12576,768]{1,0:T(8,128)} %table_grad.1, s32[8192]{0:T(1024)S(1)} %bitcast.81, bf16[8192,768]{1,0:T(8,128)(2,1)} %bitcast.65), kind=kCustom, calls=%fused_computation.10 | custom fusion | flops 12582912 | bytes 51216384 | tf_op jit(solution)/shard_map/scatter-add | solution.py:555
  (153 shorter events, 172.4 us)
Async XLA Ops:
  56.6 21.1 %collective-permute-start = (bf16[16,512,768]{2,1,0:T(8,128)(2,1)S(1)}, bf16[16,512,768]{2,1,0:T(8,128)(2,1)S(1)}, u32[]{:S(2)}, u32[]{:S(2)}) collective-permute-start(bf16[16,512,768]{2,1,0:T(8,128)(2,1)S(1)} %select_select_fusion), channel_id=1, source_target_pairs={{1,0},{3,2},{5,4},{7,6}} | collective-permute-start | bytes 37748744 | tf_op jit(solution)/shard_map/ppermute | solution.py:488
  236.5 3.6 collective-permute-start.2
  238.3 5.4 collective-permute-start.1
  240.1 50.6 %collective-permute-start.3 = (bf16[2,512,768]{2,1,0:T(8,128)(2,1)}, bf16[2,512,768]{2,1,0:T(8,128)(2,1)}, u32[]{:S(2)}, u32[]{:S(2)}) collective-permute-start(bf16[2,512,768]{2,1,0:T(8,128)(2,1)} %collective-permute-done.2), channel_id=1, source_target_pairs={{1,0},{5,4}} | collective-permute-start | bytes 4718600 | tf_op jit(solution)/shard_map/ppermute | solution.py:488
  294.0 46.3 %collective-permute-start.4 = (bf16[4,512,768]{2,1,0:T(8,128)(2,1)S(1)}, bf16[4,512,768]{2,1,0:T(8,128)(2,1)}, u32[]{:S(2)}, u32[]{:S(2)}) collective-permute-start(bf16[4,512,768]{2,1,0:T(8,128)(2,1)S(1)} %slice.98), channel_id=1, source_target_pairs={{3,1},{7,5}} | collective-permute-start | bytes 9437192 | tf_op jit(solution)/shard_map/ppermute | solution.py:488
  296.9 50.6 %collective-permute-start.5 = (bf16[4,512,768]{2,1,0:T(8,128)(2,1)S(1)}, bf16[4,512,768]{2,1,0:T(8,128)(2,1)}, u32[]{:S(2)}, u32[]{:S(2)}) collective-permute-start(bf16[4,512,768]{2,1,0:T(8,128)(2,1)S(1)} %slice.98), channel_id=1, source_target_pairs={{3,2},{7,6}} | collective-permute-start | bytes 9437192 | tf_op jit(solution)/shard_map/ppermute | solution.py:488
  340.3 7.8 collective-permute-start.6
  349.0 81.9 %collective-permute-start.7 = (bf16[5,512,768]{2,1,0:T(8,128)(2,1)}, bf16[5,512,768]{2,1,0:T(8,128)(2,1)}, u32[]{:S(2)}, u32[]{:S(2)}) collective-permute-start(bf16[5,512,768]{2,1,0:T(8,128)(2,1)} %get-tuple-element.69), channel_id=1, source_target_pairs={{3,1},{7,5}} | collective-permute-start | bytes 11796488 | tf_op jit(solution)/shard_map/ppermute | solution.py:488
  352.5 80.4 %collective-permute-start.8 = (bf16[5,512,768]{2,1,0:T(8,128)(2,1)}, bf16[5,512,768]{2,1,0:T(8,128)(2,1)}, u32[]{:S(2)}, u32[]{:S(2)}) collective-permute-start(bf16[5,512,768]{2,1,0:T(8,128)(2,1)} %get-tuple-element.69), channel_id=1, source_target_pairs={{3,2},{7,6}} | collective-permute-start | bytes 11796488 | tf_op jit(solution)/shard_map/ppermute | solution.py:488
  430.9 8.7 collective-permute-start.9
  442.6 122.1 %collective-permute-start.11 = (bf16[5,512,768]{2,1,0:T(8,128)(2,1)}, bf16[5,512,768]{2,1,0:T(8,128)(2,1)}, u32[]{:S(2)}, u32[]{:S(2)}) collective-permute-start(bf16[5,512,768]{2,1,0:T(8,128)(2,1)} %get-tuple-element.73), channel_id=1, source_target_pairs={{3,2},{7,6}} | collective-permute-start | bytes 11796488 | tf_op jit(solution)/shard_map/ppermute | solution.py:488
  445.2 99.5 %collective-permute-start.10 = (bf16[5,512,768]{2,1,0:T(8,128)(2,1)}, bf16[5,512,768]{2,1,0:T(8,128)(2,1)}, u32[]{:S(2)}, u32[]{:S(2)}) collective-permute-start(bf16[5,512,768]{2,1,0:T(8,128)(2,1)} %get-tuple-element.73), channel_id=1, source_target_pairs={{3,1},{7,5}} | collective-permute-start | bytes 11796488 | tf_op jit(solution)/shard_map/ppermute | solution.py:488
  544.7 20.1 %collective-permute-start.12 = (bf16[5,512,768]{2,1,0:T(8,128)(2,1)}, bf16[5,512,768]{2,1,0:T(8,128)(2,1)S(1)}, u32[]{:S(2)}, u32[]{:S(2)}) collective-permute-start(bf16[5,512,768]{2,1,0:T(8,128)(2,1)} %collective-permute-done.10), channel_id=1, source_target_pairs={{1,0},{5,4}} | collective-permute-start | bytes 11796488 | tf_op jit(solution)/shard_map/ppermute | solution.py:488
  720.7 151.5 %collective-permute-start.13 = (bf16[2,512,768]{2,1,0:T(8,128)(2,1)}, bf16[2,512,768]{2,1,0:T(8,128)(2,1)S(1)}, u32[]{:S(2)}, u32[]{:S(2)}) collective-permute-start(bf16[2,512,768]{2,1,0:T(8,128)(2,1)} %get-tuple-element.92), channel_id=1, source_target_pairs={{0,1},{2,3},{4,5},{6,7}} | collective-permute-start | bytes 4718600 | tf_op jit(solution)/shard_map/ppermute | solution.py:488
  789.5 163.9 %collective-permute-start.14 = (bf16[4,512,768]{2,1,0:T(8,128)(2,1)}, bf16[4,512,768]{2,1,0:T(8,128)(2,1)}, u32[]{:S(2)}, u32[]{:S(2)}) collective-permute-start(bf16[4,512,768]{2,1,0:T(8,128)(2,1)} %get-tuple-element.95), channel_id=1, source_target_pairs={{0,1},{2,3},{4,5},{6,7}} | collective-permute-start | bytes 9437192 | tf_op jit(solution)/shard_map/ppermute | solution.py:488
  872.6 108.6 %collective-permute-start.15 = (bf16[5,512,768]{2,1,0:T(8,128)(2,1)}, bf16[5,512,768]{2,1,0:T(8,128)(2,1)}, u32[]{:S(2)}, u32[]{:S(2)}) collective-permute-start(bf16[5,512,768]{2,1,0:T(8,128)(2,1)} %get-tuple-element.97), channel_id=1, source_target_pairs={{0,1},{2,3},{4,5},{6,7}} | collective-permute-start | bytes 11796488 | tf_op jit(solution)/shard_map/ppermute | solution.py:488
  958.6 31.4 %collective-permute-start.16 = (bf16[5,512,768]{2,1,0:T(8,128)(2,1)}, bf16[5,512,768]{2,1,0:T(8,128)(2,1)}, u32[]{:S(2)}, u32[]{:S(2)}) collective-permute-start(bf16[5,512,768]{2,1,0:T(8,128)(2,1)} %get-tuple-element.98), channel_id=1, source_target_pairs={{0,1},{2,3},{4,5},{6,7}} | collective-permute-start | bytes 11796488 | tf_op jit(solution)/shard_map/ppermute | solution.py:488
  998.9 186.2 %collective-permute-start.17 = (bf16[2,512,768]{2,1,0:T(8,128)(2,1)}, bf16[2,512,768]{2,1,0:T(8,128)(2,1)}, u32[]{:S(2)}, u32[]{:S(2)}) collective-permute-start(bf16[2,512,768]{2,1,0:T(8,128)(2,1)} %convert_element_type.64), channel_id=1, source_target_pairs={{1,3},{5,7}} | collective-permute-start | bytes 4718600 | tf_op jit(solution)/shard_map/ppermute | solution.py:488
  1000.8 184.3 %collective-permute-start.18 = (bf16[4,512,768]{2,1,0:T(8,128)(2,1)}, bf16[4,512,768]{2,1,0:T(8,128)(2,1)}, u32[]{:S(2)}, u32[]{:S(2)}) collective-permute-start(bf16[4,512,768]{2,1,0:T(8,128)(2,1)} %convert_element_type.67), channel_id=1, source_target_pairs={{1,3},{5,7}} | collective-permute-start | bytes 9437192 | tf_op jit(solution)/shard_map/ppermute | solution.py:488
  1003.1 182.0 %collective-permute-start.19 = (bf16[5,512,768]{2,1,0:T(8,128)(2,1)}, bf16[5,512,768]{2,1,0:T(8,128)(2,1)}, u32[]{:S(2)}, u32[]{:S(2)}) collective-permute-start(bf16[5,512,768]{2,1,0:T(8,128)(2,1)} %get-tuple-element.102), channel_id=1, source_target_pairs={{1,3},{5,7}} | collective-permute-start | bytes 11796488 | tf_op jit(solution)/shard_map/ppermute | solution.py:488
  1005.6 179.5 %collective-permute-start.20 = (bf16[5,512,768]{2,1,0:T(8,128)(2,1)}, bf16[5,512,768]{2,1,0:T(8,128)(2,1)}, u32[]{:S(2)}, u32[]{:S(2)}) collective-permute-start(bf16[5,512,768]{2,1,0:T(8,128)(2,1)} %get-tuple-element.103), channel_id=1, source_target_pairs={{1,3},{5,7}} | collective-permute-start | bytes 11796488 | tf_op jit(solution)/shard_map/ppermute | solution.py:488
  1008.4 176.7 %copy-start.3 = (f32[5,512,768]{2,1,0:T(8,128)S(1)}, f32[5,512,768]{2,1,0:T(8,128)}, u32[]{:S(2)}) copy-start(f32[5,512,768]{2,1,0:T(8,128)} %get-tuple-element.116) | copy-start | bytes 23592964
  1238.5 209.2 %copy-start.14 = (s32[1,1,16,512]{3,2,1,0:T(8,128)S(1)}, s32[1,1,16,512]{3,2,1,0:T(8,128)}, u32[]{:S(2)}) copy-start(s32[1,1,16,512]{3,2,1,0:T(8,128)} %get-tuple-element.136) | copy-start | bytes 98308
  1441.7 103.9 %collective-permute-start.21 = (bf16[16,512,768]{2,1,0:T(8,128)(2,1)}, bf16[16,512,768]{2,1,0:T(8,128)(2,1)}, u32[]{:S(2)}, u32[]{:S(2)}) collective-permute-start(bf16[16,512,768]{2,1,0:T(8,128)(2,1)} %get-tuple-element.123), channel_id=1, source_target_pairs={{0,1},{2,3},{4,5},{6,7}} | collective-permute-start | bytes 37748744 | tf_op jit(solution)/shard_map/ppermute | solution.py:488
  (23 other events, 1448.1 us)

commit v4 on v3

--- a/solution.py
+++ b/solution.py
@@ -7,6 +7,8 @@
 from jax.sharding import PartitionSpec as P
 
 NORM_EPS = 1e-6
+LOG2E = 1.4426950408889634
+LN2 = 0.6931471805599453
 GELU_K = 0.7978845608028654
 GELU_A = 0.044715
 SUB = 256
@@ -17,10 +19,12 @@
 TILE = SUB * SUBS
 CUTS = (0, 2, 6, 11, 16)
 PARTS = 6
+SPLIT = 2
 V_TILE = 640
 VMEM_CAP = 56 * 1024 * 1024
 BF = jnp.bfloat16
 F32 = jnp.float32
+NT = (((1,), (1,)), ((), ()))
 
 
 def norm_f32(act_rows):
@@ -313,16 +317,16 @@
     n_rows = n_ref[0]
     lab = lab_ref[0] - tile * TILE
     top, tot, hit = run[chunk, 0:1, :], run[chunk, 1:2, :], run[chunk, 2:3, :]
-    rows = lax.broadcasted_iota(jnp.int32, (SUB, n_rows.shape[1]), 0)
+    rows = lax.broadcasted_iota(jnp.int32, (SUB, n_rows.shape[0]), 0)
     for sub in range(SUBS):
         cut = slice(sub * SUB, (sub + 1) * SUB)
-        logit = jnp.dot(e_ref[cut, :], n_rows, preferred_element_type=F32) * scale
+        logit = lax.dot_general(e_ref[cut, :], n_rows, NT, preferred_element_type=F32) * scale
         if sub == SUBS - 1:
             logit = jnp.where(rows < n_valid - tile * TILE - sub * SUB, logit, -jnp.inf)
         hit = hit + jnp.sum(jnp.where(rows == lab - sub * SUB, logit, 0.0), axis=0, keepdims=True)
         new_top = jnp.maximum(top, jnp.max(logit, axis=0, keepdims=True))
-        expo = jnp.exp(logit - new_top)
-        tot = tot * jnp.exp(top - new_top) + jnp.sum(expo, axis=0, keepdims=True)
+        expo = jnp.exp2(logit - new_top)
+        tot = tot * jnp.exp2(top - new_top) + jnp.sum(expo, axis=0, keepdims=True)
         p_ref[0, cut, :] = expo.astype(BF)
         m_ref[0, 0, sub:sub + 1, :] = new_top
         top = new_top
@@ -354,7 +358,7 @@
 
 
 def head_forward(normed, emb_rows, labels, scale):
-    chunks, dim, rows = normed.shape
+    chunks, rows, dim = normed.shape
     n_valid = emb_rows.shape[0]
     tiles = -(-n_valid // TILE)
     padded = tiles * TILE
@@ -363,7 +367,7 @@
         functools.partial(head_forward_body, n_valid, scale),
         grid=(tiles, chunks),
         in_specs=[
-            pl.BlockSpec((1, dim, rows), lambda t, c: (c, 0, 0)),
+            pl.BlockSpec((1, rows, dim), lambda t, c: (c, 0, 0)),
             pl.BlockSpec((TILE, dim), lambda t, c: (t, 0)),
             row,
         ],
@@ -472,6 +476,32 @@
     )(*deltas, *normed)
 
 
+def norm_back_body(part_ref, near_ref, far_ref, act_ref, *refs):
+    grad = part_ref[0].astype(F32) + near_ref[0].astype(F32) + far_ref[0].astype(F32)
+    act = act_ref[0].astype(F32)
+    inv = lax.rsqrt(jnp.mean(act * act, axis=-1, keepdims=True) + NORM_EPS)
+    along = jnp.mean(act * grad, axis=-1, keepdims=True) * (inv * inv)
+    refs[-1][0] = (inv * (grad - act * along)).astype(BF)
+
+
+def norm_back(part, near, far, last_out, first, store):
+    count, rows, dim = part.shape
+    here = pl.BlockSpec((1, rows, dim), lambda c: (c, 0, 0))
+    there = pl.BlockSpec((1, rows, dim), lambda c: (c + first, 0, 0))
+    extra = [] if store is None else [store]
+    return pl.pallas_call(
+        norm_back_body,
+        grid=(count,),
+        in_specs=[here, here, here, there] + [pl.BlockSpec(memory_space=pl.ANY)] * len(extra),
+        out_specs=there,
+        out_shape=jax.ShapeDtypeStruct(last_out.shape, BF),
+        input_output_aliases={4: 0} if extra else {},
+        compiler_params=pltpu.CompilerParams(vmem_limit_bytes=VMEM_CAP),
+        cost_estimate=pl.CostEstimate(flops=20 * part.size, bytes_accessed=10 * part.size, transcendentals=0),
+        name="norm_back",
+    )(part, near, far, last_out, *extra)
+
+
 def solution(mesh):
 
     def stage_body(token_ids, label_ids, emb_rows, w_in, w_out):
@@ -497,7 +527,10 @@
         local_lab = label_ids - row_start
         labels = jnp.where((local_lab >= 0) & (local_lab < slice_rows), local_lab, -1)[:, None]
 
-        saved_in, last_out, normed = forward_pipe(chip_rows, w1, w2)
+        fine = (micro_count * SPLIT, micro_tokens // SPLIT, dim)
+        saved_in, last_out, normed = forward_pipe(chip_rows.reshape(fine), w1, w2)
+        last_out = last_out.reshape(chip_rows.shape)
+        normed = normed.reshape(chip_rows.shape)
 
         cuts = [slice(lo * unit, hi * unit) for lo, hi in zip(CUTS[:-1], CUTS[1:])]
         n_parts, expo, maxes, stats = [], [], [], []
@@ -512,7 +545,7 @@
                 relay, stats[-1] = lax.optimization_barrier((cross, stats[-1]))
             final = hop(relay, (1, 0))
             part = jnp.where(stage == 3, own, jnp.where(stage == 2, near, jnp.where(stage == 1, relay, final)))
-            res = head_forward(part.transpose(0, 2, 1), emb_rows, labels[cut], scale)
+            res = head_forward(part, emb_rows, labels[cut], scale * LOG2E)
             n_parts.append(part)
             expo.append(res[0])
             maxes.append(res[1])
@@ -520,30 +553,33 @@
 
         every = lax.all_gather(jnp.concatenate(stats), "stage")
         top = jnp.max(every[:, :, 0], axis=0)
-        denom = jnp.sum(every[:, :, 1] * jnp.exp(every[:, :, 0] - top), axis=0)
+        denom = jnp.sum(every[:, :, 1] * jnp.exp2(every[:, :, 0] - top), axis=0)
         hit = jnp.sum(every[:, :, 2], axis=0)
-        mean_loss = (jnp.sum(jnp.log(denom) + top - hit) / (micro_count * micro_tokens)).reshape(1)
+        mean_loss = (jnp.sum(jnp.log2(denom) + top - hit) * (LN2 / (micro_count * micro_tokens))).reshape(1)
         ratio = scale / denom
-        gain = ((jnp.exp(hit - top) / denom - 1.0) * scale)[:, None]
-
-        deltas, pairs = [], []
+        gain = ((jnp.exp2(hit - top) / denom - 1.0) * scale)[:, None]
+
+        deltas, parts, nears, sent = [], [], [], []
         for g, cut in enumerate(cuts):
-            coef = jnp.exp(maxes[g] - top[cut, None, None]) * ratio[cut, None, None]
+            coef = jnp.exp2(maxes[g] - top[cut, None, None]) * ratio[cut, None, None]
             delta, part = head_backward(expo[g], coef, labels[cut], gain[cut], emb_t)
             if g >= 2:
-                part, pairs[g - 2] = lax.optimization_barrier((part, pairs[g - 2]))
+                part, sent[g - 2] = lax.optimization_barrier((part, sent[g - 2]))
+            near = hop(part, (0, 1), (2, 3))
             deltas.append(delta)
-            pairs.append(part.astype(F32) + hop(part, (0, 1), (2, 3)).astype(F32))
-        sent = [pair.astype(BF) for pair in pairs]
-        deltas, sent, pairs = lax.optimization_barrier((deltas, sent, pairs))
+            parts.append(part)
+            nears.append(near)
+            sent.append((part.astype(F32) + near.astype(F32)).astype(BF))
+        deltas, sent = lax.optimization_barrier((deltas, sent))
         far = [hop(value, (1, 3)) for value in sent]
         grad_head = table_grad(deltas, n_parts, slice_rows, V_TILE)
         far, grad_head = lax.optimization_barrier((far, grad_head))
-        grad_n = jnp.concatenate([pair + value.astype(F32) for pair, value in zip(pairs, far)])
-        _, pull = jax.vjp(norm_f32, last_out)
-        grad_last = pull(grad_n)[0]
-
-        grads, hidden, grad_pre, dx_rows = backward_pipe(saved_in, grad_last, w1, w1.T, w2.T)
+        grad_last = None
+        for g, cut in enumerate(cuts):
+            grad_last = norm_back(parts[g], nears[g], far[g], last_out, cut.start, grad_last)
+
+        grads, hidden, grad_pre, dx_rows = backward_pipe(saved_in, grad_last.reshape(fine), w1, w1.T, w2.T)
+        dx_rows = dx_rows.reshape(chip_rows.shape)
 
         def flat(value):
             return value.reshape(-1, value.shape[2])

time: 1650 us -> 1540 us (0.933)
  other arithmetic: 199 us -> 138 us
  local copies, waits for them, and re-layouts: 92.7 us -> 73.2 us
    add x8 -> x0, other arithmetic: 48 us -> none  [the longest x4 24.7 us: stage_body(): pair + value.astype(F32)]
    pallas_call x0 -> x4, Pallas kernels: none -> 31.8 us  [norm_back(): pl.pallas_call(norm_back_body, grid=(count,), in_specs=[here, here, here,...]
    pallas_call x4, Pallas kernels: 292 us -> 267 us  [head_forward(): pl.pallas_call(functools.partial(head_forward_body, n_valid, scale), grid...]
    transpose x4 -> x0, local copies, waits for them, and re-layouts: 17.9 us -> none  [stage_body(): res = head_forward(part.transpose(0, 2, 1), emb_rows, labels[cut], scale)]
  transfers between devices with their start and end apart: 22 -> 22, of which waited for: 4 -> 4; matrix products, arithmetic and copies ran while one was open for 10% -> 9% of each run, Pallas kernels for 38% -> 38%
where the time goes in v4:
time: 1540 us; the launch traced here: 1530 us
  Pallas kernels  1090 us (71%)
  other arithmetic  138 us (9%)
  matrix products  97 us (6%)
  local copies, waits for them, and re-layouts  73.2 us (5%)
  waiting for transfers between devices  63.1 us (4%)
  starting transfers between devices  48.4 us (3%)
    pallas_call x4, Pallas kernels, head_forward(): pl.pallas_call(functools.partial(head_forward_body, n_valid, scale), grid...  267 us
    pallas_call x4, Pallas kernels, head_backward(): pl.pallas_call(head_backward_body, grid=(tiles, chunks), in_specs=[block,...  260 us
    pallas_call x1, Pallas kernels, backward_pipe(): pl.pallas_call(backward_pipe_body, in_specs=[any_spec] * 5, out_specs=[an...  192 us
    pallas_call x1, Pallas kernels, table_grad(): pl.pallas_call(functools.partial(table_grad_body, groups), grid=(-(-slice...  177 us
    pallas_call x1, Pallas kernels, forward_pipe(): pl.pallas_call(forward_pipe_body, in_specs=[any_spec] * 3, out_specs=[any...  149 us
    scatter-add x1, other arithmetic, stage_body(): grad_head.at[seg].add(dx_rows.reshape(-1, dim).astype(F32), mode='drop')  80.4 us
    ppermute x22, waiting for transfers between devices, hop(): return lax.ppermute(value, 'stage', pairs)  63.1 us
    dot_general x1, matrix products, stage_body(): jnp.einsum('tf,td->fd', flat(hidden), flat(grads), preferred_element_type...  48.7 us
  transfers between devices with their start and end apart: 22, of which 4 were waited for; matrix products, arithmetic and copies ran while one was open for 9% of the time, Pallas kernels for 38%

profile of v4, /device:TPU:0, one launch (start us, length us, event | category | flops | bytes accessed | tf_op | source)
XLA Modules:
  0.0 1528.2 jit_solution(5127896169808065037)
XLA Ops:
  2.8 46.0 %gather_fusion = bf16[8192,768]{1,0:T(8,128)(2,1)} fusion(bf16[12576,768]{1,0:T(8,128)(2,1)} %e_ref.9, s32[8192]{0:T(1024)S(1)} %broadcast_clamp_fusion), kind=kCustom, calls=%fused_computation | custom fusion | bytes 25198592 | tf_op jit(solution)/shard_map/jit(_take)/gather | solution.py:522
  48.9 7.7 select_select_fusion
  57.9 19.8 %collective-permute-done = bf16[16,512,768]{2,1,0:T(8,128)(2,1)S(1)} collective-permute-done((bf16[16,512,768]{2,1,0:T(8,128)(2,1)S(1)}, bf16[16,512,768]{2,1,0:T(8,128)(2,1)S(1)}, u32[]{:S(2)}, u32[]{:S(2)}) %collective-permute-start) | collective-permute-done | bytes 12582944 | tf_op jit(solution)/shard_map/ppermute | solution.py:518
  82.8 149.0 %forward_pipe.1 = (bf16[32,256,768]{2,1,0:T(8,128)(2,1)}, bf16[32,256,768]{2,1,0:T(8,128)(2,1)}, bf16[32,256,768]{2,1,0:T(8,128)(2,1)}) custom-call(bf16[32,256,768]{2,1,0:T(8,128)(2,1)} %bitcast.91, bf16[768,3072]{1,0:T(8,128)(2,1)} %bitcast.96, bf16[3072,768]{1,0:T(8,128)(2,1)} %bitcast.95), custom_call_target="tpu_custom_call" | custom-call | flops 77309411328 | bytes 9437184 | tf_op jit(solution)/shard_map/forward_pipe/pallas_call | solution.py:137
  240.9 34.0 %collective-permute-done.3 = bf16[2,512,768]{2,1,0:T(8,128)(2,1)} collective-permute-done((bf16[2,512,768]{2,1,0:T(8,128)(2,1)S(1)}, bf16[2,512,768]{2,1,0:T(8,128)(2,1)}, u32[]{:S(2)}, u32[]{:S(2)}) %collective-permute-start.3) | collective-permute-done | bytes 1572896 | tf_op jit(solution)/shard_map/ppermute | solution.py:518
  283.3 35.5 %head_fwd.4 = (bf16[2,12800,512]{2,1,0:T(8,128)(2,1)}, f32[2,5,10,512]{3,2,1,0:T(8,128)}, f32[2,3,512]{2,1,0:T(4,128)}) custom-call(bf16[2,512,768]{2,1,0:T(8,128)(2,1)} %select_select_fusion.4.n_ref.refs_4_, bf16[12576,768]{1,0:T(8,128)(2,1)} %e_ref.9, s32[2,1,512]{2,1,0:T(1,128)} %copy.37.lab_ref), custom_call_target="tpu_custom_call" | custom-call | flops 20132659200 | bytes 45875200 | tf_op jit(solution)/shard_map/head_fwd/pallas_call | solution.py:366
  334.4 66.6 %head_fwd.5 = (bf16[4,12800,512]{2,1,0:T(8,128)(2,1)}, f32[4,5,10,512]{3,2,1,0:T(8,128)}, f32[4,3,512]{2,1,0:T(4,128)}) custom-call(bf16[4,512,768]{2,1,0:T(8,128)(2,1)} %select_select_fusion.3.n_ref.refs_5_, bf16[12576,768]{1,0:T(8,128)(2,1)} %e_ref.9, s32[4,1,512]{2,1,0:T(1,128)} %copy.38.lab_ref), custom_call_target="tpu_custom_call" | custom-call | flops 40265318400 | bytes 72089600 | tf_op jit(solution)/shard_map/head_fwd/pallas_call | solution.py:366
  402.9 6.7 collective-permute-done.9
  417.8 82.2 %head_fwd.6 = (bf16[5,12800,512]{2,1,0:T(8,128)(2,1)}, f32[5,5,10,512]{3,2,1,0:T(8,128)}, f32[5,3,512]{2,1,0:T(4,128)}) custom-call(bf16[5,512,768]{2,1,0:T(8,128)(2,1)} %select_select_fusion.2.n_ref.refs_6_, bf16[12576,768]{1,0:T(8,128)(2,1)} %e_ref.9, s32[5,1,512]{2,1,0:T(1,128)} %slice.123.lab_ref), custom_call_target="tpu_custom_call" | custom-call | flops 50331648000 | bytes 85196800 | tf_op jit(solution)/shard_map/head_fwd/pallas_call | solution.py:366
  502.4 18.2 %table_t.1.et_ref = bf16[768,12800]{1,0:T(8,128)(2,1)} custom-call(bf16[12576,768]{1,0:T(8,128)(2,1)} %e_ref.9), custom_call_target="tpu_custom_call" | custom-call | flops 196608000 | bytes 39321600 | tf_op jit(solution)/shard_map/table_t/pallas_call | solution.py:348
  525.4 82.3 %head_fwd.7 = (bf16[5,12800,512]{2,1,0:T(8,128)(2,1)}, f32[5,5,10,512]{3,2,1,0:T(8,128)}, f32[5,3,512]{2,1,0:T(4,128)}) custom-call(bf16[5,512,768]{2,1,0:T(8,128)(2,1)} %select_select_fusion.1.n_ref.refs_7_, bf16[12576,768]{1,0:T(8,128)(2,1)} %e_ref.9, s32[5,1,512]{2,1,0:T(1,128)} %copy.39.lab_ref), custom_call_target="tpu_custom_call" | custom-call | flops 50331648000 | bytes 85196800 | tf_op jit(solution)/shard_map/head_fwd/pallas_call | solution.py:366
  608.6 11.7 all-gather
  623.3 65.1 %head_bwd.5 = (bf16[4,12800,512]{2,1,0:T(8,128)(2,1)}, bf16[4,512,768]{2,1,0:T(8,128)(2,1)}) custom-call(bf16[4,12800,512]{2,1,0:T(8,128)(2,1)} %get-tuple-element.78.p_ref, f32[4,5,10,512]{3,2,1,0:T(8,128)} %exponential_multiply_fusion.2.c_ref, s32[4,1,512]{2,1,0:T(1,128)} %copy.38.lab_ref, ...), custom_call_target="tpu_custom_call", output_to_operand_aliasing={{0}: (0, {})} | custom-call | flops 40265318400 | bytes 124518400 | tf_op jit(solution)/shard_map/head_bwd/pallas_call | solution.py:432
  692.3 39.1 %head_bwd.6 = (bf16[2,12800,512]{2,1,0:T(8,128)(2,1)}, bf16[2,512,768]{2,1,0:T(8,128)(2,1)}) custom-call(bf16[2,12800,512]{2,1,0:T(8,128)(2,1)} %get-tuple-element.82.p_ref, f32[2,5,10,512]{3,2,1,0:T(8,128)} %exponential_multiply_fusion.3.c_ref, s32[2,1,512]{2,1,0:T(1,128)} %copy.37.lab_ref, ...), custom_call_target="tpu_custom_call", output_to_operand_aliasing={{0}: (0, {})} | custom-call | flops 20132659200 | bytes 72089600 | tf_op jit(solution)/shard_map/head_bwd/pallas_call | solution.py:432
  734.0 77.7 %head_bwd.7 = (bf16[5,12800,512]{2,1,0:T(8,128)(2,1)}, bf16[5,512,768]{2,1,0:T(8,128)(2,1)}) custom-call(bf16[5,12800,512]{2,1,0:T(8,128)(2,1)} %get-tuple-element.86.p_ref, f32[5,5,10,512]{3,2,1,0:T(8,128)} %exponential_multiply_fusion.c_ref, s32[5,1,512]{2,1,0:T(1,128)} %slice.123.lab_ref, ...), custom_call_target="tpu_custom_call", output_to_operand_aliasing={{0}: (0, {})} | custom-call | flops 50331648000 | bytes 150732800 | tf_op jit(solution)/shard_map/head_bwd/pallas_call | solution.py:432
  817.6 77.7 %head_bwd.4 = (bf16[5,12800,512]{2,1,0:T(8,128)(2,1)}, bf16[5,512,768]{2,1,0:T(8,128)(2,1)}) custom-call(bf16[5,12800,512]{2,1,0:T(8,128)(2,1)} %get-tuple-element.75.p_ref, f32[5,5,10,512]{3,2,1,0:T(8,128)} %exponential_multiply_fusion.1.c_ref, s32[5,1,512]{2,1,0:T(1,128)} %copy.39.lab_ref, ...), custom_call_target="tpu_custom_call", output_to_operand_aliasing={{0}: (0, {})} | custom-call | flops 50331648000 | bytes 150732800 | tf_op jit(solution)/shard_map/head_bwd/pallas_call | solution.py:432
  936.2 176.6 %table_grad.1 = f32[12576,768]{1,0:T(8,128)} custom-call(bf16[2,12800,512]{2,1,0:T(8,128)(2,1)} %get-tuple-element.99.refs_0_, bf16[4,12800,512]{2,1,0:T(8,128)(2,1)} %get-tuple-element.100.refs_1_, bf16[5,12800,512]{2,1,0:T(8,128)(2,1)} %get-tuple-element.101.refs_2_, bf16[5,12800,512]{2,1,0:T(8,128)(2,1)} %get-tuple-element.102.refs_3_, ...), custom_call_target="tpu_custom_call" | custom-call | flops 158242701312 | bytes 206045184 | tf_op jit(solution)/shard_map/table_grad/pallas_call | solution.py:466
  1117.2 7.7 norm_back.5.refs_0_
  1124.9 9.8 norm_back.6.refs_0_
  1134.7 9.9 norm_back.7
  1144.6 191.8 %backward_pipe.1 = (bf16[32,256,768]{2,1,0:T(8,128)(2,1)}, bf16[32,256,3072]{2,1,0:T(8,128)(2,1)}, bf16[32,256,3072]{2,1,0:T(8,128)(2,1)}, bf16[32,256,768]{2,1,0:T(8,128)(2,1)}) custom-call(bf16[32,256,768]{2,1,0:T(8,128)(2,1)} %get-tuple-element.74.x_ref, bf16[32,256,768]{2,1,0:T(8,128)(2,1)} %bitcast.75, bf16[768,3072]{1,0:T(8,128)(2,1)} %bitcast.97, ...), custom_call_target="tpu_custom_call" | custom-call | flops 115964116992 | bytes 9437184 | tf_op jit(solution)/shard_map/backward_pipe/pallas_call | solution.py:289
  1343.4 48.3 %convolution_bitcast_fusion.1 = f32[1,768,3072]{2,1,0:T(8,128)} fusion(bf16[32,256,768]{2,1,0:T(8,128)(2,1)} %get-tuple-element.74.x_ref, bf16[32,256,3072]{2,1,0:T(8,128)(2,1)} %get-tuple-element.111), kind=kOutput, calls=%fused_computation.10 | convolution fusion | flops 38654705664 | bytes 72351744 | tf_op jit(solution)/shard_map/td,tf->df/dot_general | solution.py:587
  1391.7 48.7 %convolution_bitcast_fusion = f32[1,3072,768]{2,1,0:T(8,128)} fusion(bf16[32,256,3072]{2,1,0:T(8,128)(2,1)} %get-tuple-element.112, bf16[32,256,768]{2,1,0:T(8,128)(2,1)} %get-tuple-element.113), kind=kOutput, calls=%fused_computation.9 | convolution fusion | flops 38654705664 | bytes 72351744 | tf_op jit(solution)/shard_map/tf,td->fd/dot_general | solution.py:588
  1446.5 80.4 %scatter_custom_fusion = f32[12576,768]{1,0:T(8,128)} fusion(f32[12576,768]{1,0:T(8,128)} %table_grad.1, s32[8192]{0:T(1024)S(1)} %bitcast.104, bf16[8192,768]{1,0:T(8,128)(2,1)} %bitcast.80), kind=kCustom, calls=%fused_computation.2 | custom fusion | flops 12582912 | bytes 51216384 | tf_op jit(solution)/shard_map/scatter-add | solution.py:591
  (132 shorter events, 132.7 us)
Async XLA Ops:
  56.6 21.1 %collective-permute-start = (bf16[16,512,768]{2,1,0:T(8,128)(2,1)S(1)}, bf16[16,512,768]{2,1,0:T(8,128)(2,1)S(1)}, u32[]{:S(2)}, u32[]{:S(2)}) collective-permute-start(bf16[16,512,768]{2,1,0:T(8,128)(2,1)S(1)} %select_select_fusion), channel_id=1, source_target_pairs={{1,0},{3,2},{5,4},{7,6}} | collective-permute-start | bytes 37748744 | tf_op jit(solution)/shard_map/ppermute | solution.py:518
  233.3 2.6 collective-permute-start.2
  234.1 6.9 collective-permute-start.1
  235.9 39.1 %collective-permute-start.3 = (bf16[2,512,768]{2,1,0:T(8,128)(2,1)S(1)}, bf16[2,512,768]{2,1,0:T(8,128)(2,1)}, u32[]{:S(2)}, u32[]{:S(2)}) collective-permute-start(bf16[2,512,768]{2,1,0:T(8,128)(2,1)S(1)} %collective-permute-done.2), channel_id=1, source_target_pairs={{1,0},{5,4}} | collective-permute-start | bytes 4718600 | tf_op jit(solution)/shard_map/ppermute | solution.py:518
  277.8 41.0 %collective-permute-start.4 = (bf16[4,512,768]{2,1,0:T(8,128)(2,1)}, bf16[4,512,768]{2,1,0:T(8,128)(2,1)}, u32[]{:S(2)}, u32[]{:S(2)}) collective-permute-start(bf16[4,512,768]{2,1,0:T(8,128)(2,1)} %bitcast.6), channel_id=1, source_target_pairs={{3,1},{7,5}} | collective-permute-start | bytes 9437192 | tf_op jit(solution)/shard_map/ppermute | solution.py:518
  280.7 43.0 %collective-permute-start.5 = (bf16[4,512,768]{2,1,0:T(8,128)(2,1)}, bf16[4,512,768]{2,1,0:T(8,128)(2,1)}, u32[]{:S(2)}, u32[]{:S(2)}) collective-permute-start(bf16[4,512,768]{2,1,0:T(8,128)(2,1)} %bitcast.6), channel_id=1, source_target_pairs={{3,2},{7,6}} | collective-permute-start | bytes 9437192 | tf_op jit(solution)/shard_map/ppermute | solution.py:518
  318.8 7.6 collective-permute-start.6
  328.7 72.3 %collective-permute-start.7 = (bf16[5,512,768]{2,1,0:T(8,128)(2,1)S(1)}, bf16[5,512,768]{2,1,0:T(8,128)(2,1)}, u32[]{:S(2)}, u32[]{:S(2)}) collective-permute-start(bf16[5,512,768]{2,1,0:T(8,128)(2,1)S(1)} %bitcast.84), channel_id=1, source_target_pairs={{3,1},{7,5}} | collective-permute-start | bytes 11796488 | tf_op jit(solution)/shard_map/ppermute | solution.py:518
  331.9 71.1 %collective-permute-start.8 = (bf16[5,512,768]{2,1,0:T(8,128)(2,1)S(1)}, bf16[5,512,768]{2,1,0:T(8,128)(2,1)}, u32[]{:S(2)}, u32[]{:S(2)}) collective-permute-start(bf16[5,512,768]{2,1,0:T(8,128)(2,1)S(1)} %bitcast.85), channel_id=1, source_target_pairs={{3,2},{7,6}} | collective-permute-start | bytes 11796488 | tf_op jit(solution)/shard_map/ppermute | solution.py:518
  401.0 8.6 collective-permute-start.9
  414.3 106.3 %collective-permute-start.11 = (bf16[5,512,768]{2,1,0:T(8,128)(2,1)S(1)}, bf16[5,512,768]{2,1,0:T(8,128)(2,1)S(1)}, u32[]{:S(2)}, u32[]{:S(2)}) collective-permute-start(bf16[5,512,768]{2,1,0:T(8,128)(2,1)S(1)} %bitcast.81), channel_id=1, source_target_pairs={{3,2},{7,6}} | collective-permute-start | bytes 11796488 | tf_op jit(solution)/shard_map/ppermute | solution.py:518
  415.2 84.8 %collective-permute-start.10 = (bf16[5,512,768]{2,1,0:T(8,128)(2,1)S(1)}, bf16[5,512,768]{2,1,0:T(8,128)(2,1)}, u32[]{:S(2)}, u32[]{:S(2)}) collective-permute-start(bf16[5,512,768]{2,1,0:T(8,128)(2,1)S(1)} %bitcast.82), channel_id=1, source_target_pairs={{3,1},{7,5}} | collective-permute-start | bytes 11796488 | tf_op jit(solution)/shard_map/ppermute | solution.py:518
  500.0 20.6 %collective-permute-start.12 = (bf16[5,512,768]{2,1,0:T(8,128)(2,1)}, bf16[5,512,768]{2,1,0:T(8,128)(2,1)}, u32[]{:S(2)}, u32[]{:S(2)}) collective-permute-start(bf16[5,512,768]{2,1,0:T(8,128)(2,1)} %collective-permute-done.10), channel_id=1, source_target_pairs={{1,0},{5,4}} | collective-permute-start | bytes 11796488 | tf_op jit(solution)/shard_map/ppermute | solution.py:518
  525.4 96.8 %copy-start.6 = (f32[4,5,10,512]{3,2,1,0:T(8,128)S(1)}, f32[4,5,10,512]{3,2,1,0:T(8,128)}, u32[]{:S(2)}) copy-start(f32[4,5,10,512]{3,2,1,0:T(8,128)} %get-tuple-element.79) | copy-start | bytes 1228804
  688.4 206.9 %collective-permute-start.13 = (bf16[4,512,768]{2,1,0:T(8,128)(2,1)}, bf16[4,512,768]{2,1,0:T(8,128)(2,1)S(1)}, u32[]{:S(2)}, u32[]{:S(2)}) collective-permute-start(bf16[4,512,768]{2,1,0:T(8,128)(2,1)} %get-tuple-element.80.part_ref), channel_id=1, source_target_pairs={{0,1},{2,3},{4,5},{6,7}} | collective-permute-start | bytes 9437192 | tf_op jit(solution)/shard_map/ppermute | solution.py:518
  731.4 81.3 %collective-permute-start.15 = (bf16[2,512,768]{2,1,0:T(8,128)(2,1)}, bf16[2,512,768]{2,1,0:T(8,128)(2,1)S(1)}, u32[]{:S(2)}, u32[]{:S(2)}) collective-permute-start(bf16[2,512,768]{2,1,0:T(8,128)(2,1)} %get-tuple-element.91.part_ref), channel_id=1, source_target_pairs={{0,1},{2,3},{4,5},{6,7}} | collective-permute-start | bytes 4718600 | tf_op jit(solution)/shard_map/ppermute | solution.py:518
  814.5 99.8 %collective-permute-start.16 = (bf16[5,512,768]{2,1,0:T(8,128)(2,1)}, bf16[5,512,768]{2,1,0:T(8,128)(2,1)}, u32[]{:S(2)}, u32[]{:S(2)}) collective-permute-start(bf16[5,512,768]{2,1,0:T(8,128)(2,1)} %get-tuple-element.94.part_ref), channel_id=1, source_target_pairs={{0,1},{2,3},{4,5},{6,7}} | collective-permute-start | bytes 11796488 | tf_op jit(solution)/shard_map/ppermute | solution.py:518
  897.9 22.6 %collective-permute-start.14 = (bf16[5,512,768]{2,1,0:T(8,128)(2,1)}, bf16[5,512,768]{2,1,0:T(8,128)(2,1)}, u32[]{:S(2)}, u32[]{:S(2)}) collective-permute-start(bf16[5,512,768]{2,1,0:T(8,128)(2,1)} %get-tuple-element.81.part_ref), channel_id=1, source_target_pairs={{0,1},{2,3},{4,5},{6,7}} | collective-permute-start | bytes 11796488 | tf_op jit(solution)/shard_map/ppermute | solution.py:518
  926.6 186.1 %collective-permute-start.17 = (bf16[2,512,768]{2,1,0:T(8,128)(2,1)}, bf16[2,512,768]{2,1,0:T(8,128)(2,1)}, u32[]{:S(2)}, u32[]{:S(2)}) collective-permute-start(bf16[2,512,768]{2,1,0:T(8,128)(2,1)} %add_convert_fusion.3), channel_id=1, source_target_pairs={{1,3},{5,7}} | collective-permute-start | bytes 4718600 | tf_op jit(solution)/shard_map/ppermute | solution.py:518
  928.5 184.2 %collective-permute-start.18 = (bf16[4,512,768]{2,1,0:T(8,128)(2,1)}, bf16[4,512,768]{2,1,0:T(8,128)(2,1)}, u32[]{:S(2)}, u32[]{:S(2)}) collective-permute-start(bf16[4,512,768]{2,1,0:T(8,128)(2,1)} %add_convert_fusion.2), channel_id=1, source_target_pairs={{1,3},{5,7}} | collective-permute-start | bytes 9437192 | tf_op jit(solution)/shard_map/ppermute | solution.py:518
  930.9 181.9 %collective-permute-start.19 = (bf16[5,512,768]{2,1,0:T(8,128)(2,1)}, bf16[5,512,768]{2,1,0:T(8,128)(2,1)}, u32[]{:S(2)}, u32[]{:S(2)}) collective-permute-start(bf16[5,512,768]{2,1,0:T(8,128)(2,1)} %add_convert_fusion.1), channel_id=1, source_target_pairs={{1,3},{5,7}} | collective-permute-start | bytes 11796488 | tf_op jit(solution)/shard_map/ppermute | solution.py:518
  933.5 179.3 %collective-permute-start.20 = (bf16[5,512,768]{2,1,0:T(8,128)(2,1)}, bf16[5,512,768]{2,1,0:T(8,128)(2,1)}, u32[]{:S(2)}, u32[]{:S(2)}) collective-permute-start(bf16[5,512,768]{2,1,0:T(8,128)(2,1)} %add_convert_fusion), channel_id=1, source_target_pairs={{1,3},{5,7}} | collective-permute-start | bytes 11796488 | tf_op jit(solution)/shard_map/ppermute | solution.py:518
  1144.6 198.0 %copy-start.8 = (s32[1,1,16,512]{3,2,1,0:T(8,128)S(1)}, s32[1,1,16,512]{3,2,1,0:T(8,128)}, u32[]{:S(2)}) copy-start(s32[1,1,16,512]{3,2,1,0:T(8,128)} %get-tuple-element.122) | copy-start | bytes 98308
  1336.4 104.0 %collective-permute-start.21 = (bf16[16,512,768]{2,1,0:T(8,128)(2,1)}, bf16[16,512,768]{2,1,0:T(8,128)(2,1)}, u32[]{:S(2)}, u32[]{:S(2)}) collective-permute-start(bf16[16,512,768]{2,1,0:T(8,128)(2,1)} %bitcast.87), channel_id=1, source_target_pairs={{0,1},{2,3},{4,5},{6,7}} | collective-permute-start | bytes 37748744 | tf_op jit(solution)/shard_map/ppermute | solution.py:518
  (17 other events, 869.0 us)
